TPU v7x, 32 devices: a whole 2x2x4 slice. The times are simulated.
32 devices in a mesh: expert: 8 (over z, y), vocab: 4 (over x, core).
Axes of the slice: x: 2, y: 2, z: 4, core: 2. Of those that a mesh axis runs over, the one named last changes fastest.
Arguments:
- layer_out: bfloat16 [256, 2048], P('expert'), may hold values from -6 to 6
- moe_input: bfloat16 [256, 2048], P('expert'), may hold values from -6 to 6
- final_gain: float32 [2048], replicated, may hold values from 0.1 to 1.9
- head_weight: bfloat16 [2048, 12288], P(None, ('expert', 'vocab')), may hold values from -0.125 to 0.125
- clean_ids: int32 [256], P('expert'), may hold values from 0 to 12287
- levels: int32 [256], P('expert'), may hold values from 0 to 15
- ratio_table: float32 [16], replicated, may hold values from 0.5 to 8
- gate_weights: float32 [256, 8], P('expert'), may hold values from 0.05 to 0.5
- expert_ids: int32 [256, 8], P('expert'), may hold values from 0 to 15, all different within a row; in each aligned block of 32 rows (0 to 31, 32 to 63, ...) at most 32 rows name the same one
- w_gate: bfloat16 [16, 2048, 1024], P('expert', None, 'vocab'), may hold values from -0.125 to 0.125
- w_up: bfloat16 [16, 2048, 1024], P('expert', None, 'vocab'), may hold values from -0.125 to 0.125
- w_down: bfloat16 [16, 1024, 2048], P('expert', 'vocab'), may hold values from -0.1875 to 0.1875
Outputs:
- head_grad: float32 [2048, 12288], P(None, ('expert', 'vocab'))
- residual_grad: float32 [256, 2048], P('expert', 'vocab')
- input_grad: float32 [256, 2048], P('expert', 'vocab')
Inputs may be any that keep to these rules, and one draw needn't show every extreme that they name: `expert_ids`: the 8 experts of a row are distinct; among the 32 rows of one index of expert no expert is named by more than 32 rows.
All inputs are finite; a program needn't handle non-finite values.
Results may differ from a plain program's by a relative error of at most 0.0044.
The roundings to bfloat16 on the way count: a program that leaves them out, or rounds other values in their place, can miss the bound.
Values may be sent and summed in bfloat16 or wider, within the bound.
A program may use at most 64 MiB of HBM per device.

v0:
```python
import functools
import math

import jax
import jax.numpy as jnp
from jax import lax
from jax.experimental import pallas as pl
from jax.experimental.pallas import tpu as pltpu
from jax.sharding import PartitionSpec as P

epsilon = 1e-05
CORES = 2
PAIR = 2
MESH = pl.DeviceIdType.MESH
VMEM = pl.BlockSpec(memory_space=pltpu.VMEM)


def place():
    e, v = lax.axis_index("expert"), lax.axis_index("vocab")
    n_expert, n_vocab = lax.axis_size("expert"), lax.axis_size("vocab")
    return e, v // CORES, v % CORES, n_expert, n_vocab // CORES


def device(e, a, c):
    return (e, a * CORES + c)


def greet(devices):
    barrier = pltpu.get_barrier_semaphore()
    for other in devices:
        pl.semaphore_signal(barrier, inc=1, device_id=other, device_id_type=MESH)
    pl.semaphore_wait(barrier, len(devices))


def remote(src, dst, send, recv, target):
    return pltpu.make_async_remote_copy(
        src_ref=src, dst_ref=dst, send_sem=send, recv_sem=recv, device_id=target,
        device_id_type=MESH,
    )


def gather_kernel(n_data, n_meta, *refs):
    count = n_data + n_meta
    ins, outs = refs[:count], refs[count:2 * count]
    local_sem, e_send, e_recv, a_send, a_recv, c_send, c_recv, m_send, m_recv = refs[2 * count:]
    e, a, c, n_e, n_a = place()
    n_o = n_e // PAIR
    o, inner = e // PAIR, e % PAIR
    outer_peer = [device(lax.rem(o + d, n_o) * PAIR + inner, a, c) for d in range(1, n_o)]
    inner_peer = device(o * PAIR + 1 - inner, a, c)
    chip_peer = [device(e, lax.rem(a + d, n_a), c) for d in range(1, n_a)]
    sibling = device(e, a, 1 - c)
    greet(outer_peer + [inner_peer] + chip_peer + [sibling])
    share = ins[0].shape[1]

    def source(b):
        across, d = b // n_o, b % n_o
        return lax.rem(o + n_o - d, n_o) * PAIR + (1 - inner if across else inner)

    def block(i, b, ab, cb):
        start = pl.multiple_of((ab * CORES + cb) * share, share)
        return outs[i].at[source(b), :, pl.ds(start, share)]

    sends, locals_ = [], []

    def start(*args):
        copy = remote(*args)
        copy.start()
        sends.append(copy)

    def landed(ref, recv):
        remote(ref, ref, recv, recv, sibling).wait_recv()

    for m in range(n_meta):
        for d in range(1, n_o):
            start(ins[n_data + m], outs[n_data + m].at[e], m_send.at[m, d], m_recv.at[m, d],
                  outer_peer[d - 1])
    for i in range(count):
        slot = block(i, 0, a, c) if i < n_data else outs[i].at[e]
        if i < n_data:
            for d in range(1, n_o):
                start(ins[i], slot, e_send.at[i, d], e_recv.at[i, d], outer_peer[d - 1])
        own = pltpu.make_async_copy(ins[i], slot, local_sem.at[i])
        own.start()
        locals_.append(own)
    for m in range(n_meta):
        for d in range(n_o):
            slot = outs[n_data + m].at[source(d)]
            if d:
                landed(slot, m_recv.at[m, d])
            start(slot if d else ins[n_data + m], slot, m_send.at[m, n_o + d],
                  m_recv.at[m, n_o + d], inner_peer)
    for i in range(n_data):
        for b in range(n_e):
            mine = block(i, b, a, c)
            if b:
                landed(mine, e_recv.at[i, b])
            src = mine if b else ins[i]
            if b < n_o:
                start(src, mine, e_send.at[i, n_o + b], e_recv.at[i, n_o + b], inner_peer)
            for da in range(1, n_a):
                start(src, mine, a_send.at[i, b, da], a_recv.at[i, b, da], chip_peer[da - 1])
            start(src, mine, c_send.at[i, b, 0], c_recv.at[i, b, 0], sibling)
    for i in range(n_data):
        for b in range(n_e):
            for da in range(1, n_a):
                other = block(i, b, lax.rem(a + n_a - da, n_a), c)
                landed(other, a_recv.at[i, b, da])
                start(other, other, c_send.at[i, b, da], c_recv.at[i, b, da], sibling)
    for own in locals_:
        own.wait()
    for m in range(n_meta):
        for d in range(n_o):
            landed(outs[n_data + m].at[source(n_o + d)], m_recv.at[m, n_o + d])
    for i in range(n_data):
        for b in range(n_e):
            for da in range(n_a):
                landed(block(i, b, lax.rem(a + n_a - da, n_a), 1 - c), c_recv.at[i, b, da])
    for copy in sends:
        copy.wait_send()


def gather_all(data, meta, collective_id):
    n_e, n_a = lax.axis_size("expert"), lax.axis_size("vocab") // CORES
    n_data, n_meta = len(data), len(meta)
    width = data[0].shape[1] * n_a * CORES
    out_shape = [jax.ShapeDtypeStruct((n_e, x.shape[0], width), x.dtype) for x in data]
    out_shape += [jax.ShapeDtypeStruct((n_e, *x.shape), x.dtype) for x in meta]
    dma = pltpu.SemaphoreType.DMA
    more = max(n_meta, 1)
    outs = pl.pallas_call(
        functools.partial(gather_kernel, n_data, n_meta),
        out_shape=out_shape,
        in_specs=[VMEM] * (n_data + n_meta),
        out_specs=[VMEM] * (n_data + n_meta),
        scratch_shapes=[
            dma((n_data + n_meta,)),
            dma((n_data, n_e)), dma((n_data, n_e)),
            dma((n_data, n_e, n_a)), dma((n_data, n_e, n_a)),
            dma((n_data, n_e, n_a)), dma((n_data, n_e, n_a)),
            dma((more, n_e)), dma((more, n_e)),
        ],
        compiler_params=pltpu.CompilerParams(collective_id=collective_id, has_side_effects=True),
    )(*data, *meta)
    return [x.reshape(-1, x.shape[-1]) for x in outs]


def swap_kernel(kind, n, x_ref, y_ref, send, recv):
    e, a, c, _, _ = place()
    me = {"expert": e, "chip": a, "vocab": a * CORES + c}[kind]
    others = [lax.rem(me + d, n) for d in range(1, n)]

    def at(p):
        if kind == "expert":
            return device(p, a, c)
        return device(e, p, c) if kind == "chip" else (e, p)

    greet([at(p) for p in others])
    copies = []
    for d, p in enumerate(others):
        src = x_ref if kind == "vocab" else x_ref.at[p]
        copy = remote(src, y_ref.at[d], send.at[d], recv.at[d], at(p))
        copy.start()
        copies.append(copy)
    for copy in copies:
        copy.wait()


def swap(x, kind, n, collective_id):
    block = x.shape if kind == "vocab" else x.shape[1:]
    dma = pltpu.SemaphoreType.DMA
    return pl.pallas_call(
        functools.partial(swap_kernel, kind, n),
        out_shape=jax.ShapeDtypeStruct((n - 1, *block), x.dtype),
        in_specs=[VMEM],
        out_specs=VMEM,
        scratch_shapes=[dma((n - 1,)), dma((n - 1,))],
        compiler_params=pltpu.CompilerParams(collective_id=collective_id, has_side_effects=True),
    )(x)


def scatter_kernel(x_ref, y_ref, from_core, to_chip, from_chip, own, to_row, from_row,
                   core_send, core_recv, chip_send, chip_recv, row_send, row_recv):
    e, a, c, n_e, n_a = place()
    rows, share = y_ref.shape
    sibling = device(e, a, 1 - c)
    chip_at = [lax.rem(a + d, n_a) for d in range(n_a)]
    row_at = [lax.rem(e + d, n_e) for d in range(n_e)]
    greet([sibling] + [device(e, p, c) for p in chip_at[1:]]
          + [device(p, a, c) for p in row_at[1:]])
    order = list(range(1, n_e)) + [0]
    sends = []

    def piece(s, k, cb):
        row = pl.multiple_of(row_at[s] * rows, rows)
        column = pl.multiple_of((chip_at[k] * CORES + cb) * share, share)
        return pl.ds(row, rows), pl.ds(column, share)

    def core_copy(s, k):
        return remote(x_ref.at[piece(s, k, 1 - c)], from_core.at[s, k], core_send.at[s, k],
                      core_recv.at[s, k], sibling)

    def chip_copy(s, k):
        return remote(to_chip.at[s, k], from_chip.at[s, k], chip_send.at[s, k],
                      chip_recv.at[s, k], device(e, chip_at[k], c))

    def row_copy(s):
        return remote(to_row.at[s], from_row.at[s], row_send.at[s], row_recv.at[s],
                      device(row_at[s], a, c))

    def start(copy):
        copy.start()
        sends.append(copy)

    turns = list(range(1, n_a)) + [0]
    for s in order:
        for k in turns:
            start(core_copy(s, k))

    def first(s):
        for k in turns:
            core_copy(s, k).wait_recv()
            term = x_ref[piece(s, k, c)] + from_core[s, k]
            if k:
                to_chip[s, k] = term.astype(to_chip.dtype)
                start(chip_copy(s, k))
            else:
                own[s] = term

    def second(s):
        term = own[s]
        for k in range(1, n_a):
            chip_copy(s, k).wait_recv()
            term = term + from_chip[s, k].astype(jnp.float32)
        if s:
            to_row[s] = term.astype(to_row.dtype)
            start(row_copy(s))
        else:
            y_ref[...] = term

    lag = 2
    for step in range(n_e + lag):
        if step < n_e:
            first(order[step])
        if step >= lag:
            second(order[step - lag])
    for s in range(1, n_e):
        row_copy(s).wait_recv()
        y_ref[...] += from_row[s].astype(jnp.float32)
    for copy in sends:
        copy.wait_send()


def scatter_sum(partial, chip_type, row_type, collective_id):
    n_e, n_a = lax.axis_size("expert"), lax.axis_size("vocab") // CORES
    rows, share = partial.shape[0] // n_e, partial.shape[1] // (n_a * CORES)
    dma = pltpu.SemaphoreType.DMA
    return pl.pallas_call(
        scatter_kernel,
        out_shape=jax.ShapeDtypeStruct((rows, share), jnp.float32),
        in_specs=[VMEM],
        out_specs=VMEM,
        scratch_shapes=[
            pltpu.VMEM((n_e, n_a, rows, share), jnp.float32),
            pltpu.VMEM((n_e, n_a, rows, share), chip_type),
            pltpu.VMEM((n_e, n_a, rows, share), chip_type),
            pltpu.VMEM((n_e, rows, share), jnp.float32),
            pltpu.VMEM((n_e, rows, share), row_type),
            pltpu.VMEM((n_e, rows, share), row_type),
            dma((n_e, n_a)), dma((n_e, n_a)), dma((n_e, n_a)), dma((n_e, n_a)),
            dma((n_e,)), dma((n_e,)),
        ],
        compiler_params=pltpu.CompilerParams(collective_id=collective_id, has_side_effects=True),
    )(partial)


def on_device(
    layer_out,
    moe_input,
    final_gain,
    head_weight,
    clean_ids,
    levels,
    ratio_table,
    gate_weights,
    expert_ids,
    w_gate,
    w_up,
    w_down,
):
    rows_local, model_width = layer_out.shape
    n_expert = lax.axis_size("expert")
    n_vocab = lax.axis_size("vocab")
    expert_at, vocab_at = lax.axis_index("expert"), lax.axis_index("vocab")
    total_rows = rows_local * n_expert
    local_experts = w_gate.shape[0]
    experts_all = local_experts * n_expert
    share = model_width // n_vocab
    vocab_local = head_weight.shape[1]

    def own_share(x, axis):
        return lax.dynamic_slice_in_dim(x, vocab_at * share, share, axis)

    values = layer_out.astype(jnp.float32)
    row_scale = jnp.sqrt(jnp.mean(values * values, axis=1, keepdims=True) + epsilon)
    unit_share = own_share(layer_out, 1).astype(jnp.float32) / row_scale
    gain_share = own_share(final_gain, 0)[None, :]
    normed_share = (unit_share * gain_share).astype(jnp.bfloat16)
    labels = jnp.arange(experts_all, dtype=jnp.int32)
    gates = jnp.sum(
        jnp.where(expert_ids[:, :, None] == labels, gate_weights[:, :, None], 0.0), axis=1
    )
    level_labels = jnp.arange(ratio_table.shape[0], dtype=jnp.int32)
    ratio_rows = jnp.sum(
        jnp.where(levels[:, None] == level_labels[None, :], ratio_table[None, :], 0.0),
        axis=1, keepdims=True,
    )
    meta = jnp.concatenate([gates, ratio_rows, clean_ids[:, None].astype(jnp.float32)], axis=1)
    meta = jnp.pad(meta, ((0, 0), (0, -meta.shape[1] % 128)))
    normed_all, input_all, meta_all = gather_all(
        [normed_share, own_share(moe_input, 1)], [meta], 0
    )
    ratio_all = meta_all[:, experts_all:experts_all + 1]
    clean_all = meta_all[:, experts_all + 1:experts_all + 2].astype(jnp.int32)
    gate_all = lax.dynamic_slice_in_dim(meta_all, expert_at * local_experts, local_experts, 1)

    column_start = (expert_at * n_vocab + vocab_at) * vocab_local
    columns = column_start + jnp.arange(vocab_local, dtype=jnp.int32)
    scores = jnp.dot(normed_all, head_weight, preferred_element_type=jnp.float32)
    target_hit = (clean_all == columns[None, :]).astype(jnp.float32)
    loss_scale = 1.0 / math.sqrt(total_rows)
    score_grad = ((jnp.exp(scores) - ratio_all * target_hit) * loss_scale).astype(jnp.bfloat16)
    head_grad = lax.dot_general(
        normed_all, score_grad, (((0,), (0,)), ((), ())), preferred_element_type=jnp.float32
    )
    partial_grad = lax.dot_general(
        score_grad, head_weight, (((1,), (1,)), ((), ())), preferred_element_type=jnp.float32
    )
    normed_grad = scatter_sum(partial_grad, jnp.float32, jnp.bfloat16, 1)
    gained = gain_share * normed_grad
    mean_part = jnp.sum(unit_share * gained, axis=1, keepdims=True) / model_width
    mean_part = jnp.broadcast_to(mean_part, (rows_local, 128))
    mean_row = mean_part + jnp.sum(swap(mean_part, "vocab", n_vocab, 4), axis=0)
    residual_grad = (gained - unit_share * mean_row[:, :1]) / row_scale
    (residual_all,) = gather_all([residual_grad.astype(jnp.bfloat16)], [], 5)

    partial_input = None
    for i in range(local_experts):
        gate_pre = jnp.dot(input_all, w_gate[i], preferred_element_type=jnp.float32)
        up_pre = jnp.dot(input_all, w_up[i], preferred_element_type=jnp.float32)
        act_grad = gate_all[:, i:i + 1] * lax.dot_general(
            residual_all, w_down[i], (((1,), (1,)), ((), ())), preferred_element_type=jnp.float32
        )
        s = jax.nn.sigmoid(gate_pre)
        gate_grad = (act_grad * up_pre * s * (1.0 + gate_pre * (1.0 - s))).astype(jnp.bfloat16)
        up_grad = (act_grad * gate_pre * s).astype(jnp.bfloat16)
        for grad, weight in ((gate_grad, w_gate[i]), (up_grad, w_up[i])):
            term = lax.dot_general(
                grad, weight, (((1,), (1,)), ((), ())), preferred_element_type=jnp.float32
            )
            partial_input = term if partial_input is None else partial_input + term
    input_grad = scatter_sum(partial_input, jnp.float32, jnp.float32, 6)
    return (head_grad, residual_grad, input_grad)


def solution(mesh):
    in_specs = (
        P("expert", None),
        P("expert", None),
        P(),
        P(None, ("expert", "vocab")),
        P("expert"),
        P("expert"),
        P(),
        P("expert", None),
        P("expert", None),
        P("expert", None, "vocab"),
        P("expert", None, "vocab"),
        P("expert", "vocab", None),
    )
    out_specs = (P(None, ("expert", "vocab")), P("expert", "vocab"), P("expert", "vocab"))
    return jax.shard_map(
        on_device, mesh=mesh, in_specs=in_specs, out_specs=out_specs, check_vma=False
    )
```

profile of v0, /device:TPU:0, one launch (start us, length us, event | category | flops | bytes accessed | tf_op | source)
XLA Modules:
  0.0 138.5 jit_solution(6203691536811123030)
XLA Ops:
  0.7 0.9 dynamic_slice.13
  1.5 1.0 multiply_reduce_fusion
  2.6 1.5 %multiply_convert_fusion.4.refs_0_ = bf16[32,512]{1,0:T(8,128)(2,1)} fusion(f32[512]{0:T(512)S(1)} %dynamic_slice.13, f32[32]{0:T(128)S(1)} %add_sqrt_fusion, bf16[32,2048]{1,0:T(8,128)(2,1)} %param.12, s32[]{:T(128)S(6)} %select_n.16), kind=kLoop, calls=%fused_computation.60 | loop fusion | flops 65536 | bytes 67716 | tf_op jit(solution)/shard_map/convert_element_type | solution.py:308
  4.0 1.4 constant_dynamic-slice_fusion.2.refs_1_
  5.4 0.7 select_reduce_fusion
  6.2 0.8 select_reduce_fusion.1
  7.0 0.1 copy.27
  7.1 0.7 convert_bitcast_fusion
  7.8 0.7 select_maximum_fusion.refs_2_
  8.5 27.3 %shard_map.139 = (bf16[8,32,2048]{2,1,0:T(8,128)(2,1)}, bf16[8,32,2048]{2,1,0:T(8,128)(2,1)}, f32[8,32,128]{2,1,0:T(8,128)}) custom-call(bf16[32,512]{1,0:T(8,128)(2,1)} %multiply_convert_fusion.4.refs_0_, bf16[32,512]{1,0:T(8,128)(2,1)} %constant_dynamic-slice_fusion.2.refs_1_, f32[32,128]{1,0:T(8,128)} %select_maximum_fusion.refs_2_), custom_call_target="tpu_custom_call" | custom-call | tf_op jit(solution)/shard_map/pallas_call | solution.py:131
  35.8 1.3 constant_dynamic-slice_fusion.1
  37.3 2.0 %fusion.2 = bf16[256,384]{1,0:T(8,128)(2,1)S(1)} fusion(bf16[256,2048]{1,0:T(8,128)(2,1)} %bitcast.55, bf16[2048,384]{1,0:T(8,128)(2,1)S(1)} %copy-done, f32[256]{0:T(256)S(1)} %bitcast.61, s32[384]{0:T(512)S(1)} %iota_add_fusion, s32[256]{0:T(256)S(1)} %bitcast.60), kind=kOutput, calls=%fused_computation.6 | convolution fusion | flops 403144704 | bytes 2821632 | tf_op jit(solution)/shard_map/dot_general | solution.py:329
  39.2 2.1 %fusion.53.x_ref = f32[256,2048]{1,0:T(8,128)} fusion(bf16[256,384]{1,0:T(8,128)(2,1)S(1)} %fusion.2, bf16[2048,384]{1,0:T(8,128)(2,1)S(1)} %copy-done), kind=kOutput, calls=%fused_computation.82 | convolution fusion | flops 402653184 | bytes 3866624 | tf_op jit(solution)/shard_map/dot_general | solution.py:336
  41.3 22.4 %shard_map.140 = f32[32,512]{1,0:T(8,128)} custom-call(f32[256,2048]{1,0:T(8,128)} %fusion.53.x_ref), custom_call_target="tpu_custom_call" | custom-call | tf_op jit(solution)/shard_map/pallas_call | solution.py:258
  63.7 1.0 multiply_reduce_fusion.1
  64.7 0.7 broadcast_in_dim.48.x_ref
  65.4 5.1 %shard_map.141 = f32[3,32,128]{2,1,0:T(8,128)} custom-call(f32[32,128]{1,0:T(8,128)} %broadcast_in_dim.48.x_ref), custom_call_target="tpu_custom_call" | custom-call | tf_op jit(solution)/shard_map/pallas_call | solution.py:172
  70.5 0.8 reduce_sum.49
  71.4 0.2 fusion.46
  71.5 1.7 %fusion.51 = (bf16[32,512]{1,0:T(8,128)(2,1)}, f32[32,512]{1,0:T(8,128)}) fusion(f32[32]{0:T(128)S(1)} %fusion.46, f32[32]{0:T(128)S(1)} %add_sqrt_fusion, bf16[32,2048]{1,0:T(8,128)(2,1)S(1)} %copy-done.5, s32[]{:T(128)S(6)} %select_n.16, f32[32,512]{1,0:T(8,128)} %shard_map.140, f32[512]{0:T(512)S(1)} %dynamic_slice.13), kind=kLoop, calls=%fused_computation.80 | loop fusion | flops 114688 | bytes 198916 | tf_op jit(solution)/shard_map/convert_element_type | solution.py:345
  73.2 17.0 %shard_map.142 = bf16[8,32,2048]{2,1,0:T(8,128)(2,1)} custom-call(bf16[32,512]{1,0:T(8,128)(2,1)} %get-tuple-element.9.refs_0_), custom_call_target="tpu_custom_call" | custom-call | tf_op jit(solution)/shard_map/pallas_call | solution.py:131
  90.3 2.2 %convolution_multiply_fusion.3 = f32[256,256]{1,0:T(8,128)S(1)} fusion(bf16[256,2048]{1,0:T(8,128)(2,1)} %bitcast.58, bf16[2,256,2048]{2,1,0:T(8,128)(2,1)} %param.23, f32[256]{0:T(256)S(1)} %bitcast.63), kind=kOutput, calls=%fused_computation.14 | convolution fusion | flops 268500992 | bytes 2360320 | tf_op jit(solution)/shard_map/dot_general | solution.py:351
  92.5 0.4 fusion.18
  93.0 4.1 %fusion.9 = f32[256,2048]{1,0:T(8,128)} fusion(f32[256,256]{1,0:T(8,128)S(1)} %convolution_multiply_fusion.3, bf16[256,2048]{1,0:T(8,128)(2,1)S(1)} %bitcast.52, bf16[2,2048,256]{2,1,0:T(8,128)(2,1)} %param.21, bf16[2,2048,256]{2,1,0:T(8,128)(2,1)} %param.22, f32[256,256]{1,0:T(8,128)S(1)} %fusion.18), kind=kOutput, calls=%fused_computation.17 | convolution fusion | flops 537526272 | bytes 5767168 | tf_op jit(solution)/shard_map/dot_general | solution.py:358
  97.1 3.7 %convolution_add_fusion.2 = f32[256,2048]{1,0:T(8,128)} fusion(f32[256,2048]{1,0:T(8,128)} %fusion.9, bf16[2,2048,256]{2,1,0:T(8,128)(2,1)} %param.22, f32[256,256]{1,0:T(8,128)S(1)} %convolution_multiply_fusion.3, f32[256,256]{1,0:T(8,128)S(1)} %fusion.18), kind=kOutput, calls=%fused_computation.2 | convolution fusion | flops 269352960 | bytes 5767168 | tf_op jit(solution)/shard_map/dot_general | solution.py:358
  100.9 2.2 %convolution_multiply_fusion.1 = f32[256,256]{1,0:T(8,128)S(1)} fusion(bf16[256,2048]{1,0:T(8,128)(2,1)} %bitcast.59, bf16[2,256,2048]{2,1,0:T(8,128)(2,1)} %param.23, f32[256]{0:T(256)S(1)} %bitcast.62), kind=kOutput, calls=%fused_computation.10 | convolution fusion | flops 268500992 | bytes 2360320 | tf_op jit(solution)/shard_map/dot_general | solution.py:351
  103.1 0.4 fusion.11
  103.6 4.8 %convolution_add_fusion.1 = f32[256,2048]{1,0:T(8,128)} fusion(f32[256,2048]{1,0:T(8,128)} %convolution_add_fusion.2, f32[256,256]{1,0:T(8,128)S(1)} %convolution_multiply_fusion.1, bf16[256,2048]{1,0:T(8,128)(2,1)S(1)} %bitcast.54, bf16[2,2048,256]{2,1,0:T(8,128)(2,1)} %param.21, bf16[2,2048,256]{2,1,0:T(8,128)(2,1)} %param.22, f32[256,256]{1,0:T(8,128)S(1)} %fusion.11), kind=kOutput, calls=%fused_computation.1 | convolution fusion | flops 538050560 | bytes 7864320 | tf_op jit(solution)/shard_map/dot_general | solution.py:358
  108.4 3.7 %convolution_add_fusion.x_ref = f32[256,2048]{1,0:T(8,128)} fusion(f32[256,2048]{1,0:T(8,128)} %convolution_add_fusion.1, bf16[2,2048,256]{2,1,0:T(8,128)(2,1)} %param.22, f32[256,256]{1,0:T(8,128)S(1)} %convolution_multiply_fusion.1, f32[256,256]{1,0:T(8,128)S(1)} %fusion.11), kind=kOutput, calls=%fused_computation | convolution fusion | flops 269352960 | bytes 5767168 | tf_op jit(solution)/shard_map/dot_general | solution.py:358
  112.1 23.3 %shard_map.143 = f32[32,512]{1,0:T(8,128)} custom-call(f32[256,2048]{1,0:T(8,128)} %convolution_add_fusion.x_ref), custom_call_target="tpu_custom_call" | custom-call | tf_op jit(solution)/shard_map/pallas_call | solution.py:258
  135.5 2.4 %fusion.52 = f32[2048,384]{1,0:T(8,128)} fusion(bf16[256,2048]{1,0:T(8,128)(2,1)S(1)} %bitcast.56, bf16[256,384]{1,0:T(8,128)(2,1)S(1)} %fusion.2), kind=kOutput, calls=%fused_computation.81 | convolution fusion | flops 402653184 | bytes 4390912 | tf_op jit(solution)/shard_map/dot_general | solution.py:333
  137.9 0.6 copy.39
  (23 shorter events, 0.6 us)
Async XLA Ops:
  0.6 36.6 %copy-start = (bf16[2048,384]{1,0:T(8,128)(2,1)S(1)}, bf16[2048,384]{1,0:T(8,128)(2,1)}, u32[]{:S(2)}) copy-start(bf16[2048,384]{1,0:T(8,128)(2,1)} %param.15) | copy-start | bytes 4718596
  39.2 24.4 %copy-start.5 = (bf16[32,2048]{1,0:T(8,128)(2,1)S(1)}, bf16[32,2048]{1,0:T(8,128)(2,1)}, u32[]{:S(2)}) copy-start(bf16[32,2048]{1,0:T(8,128)(2,1)} %param.12) | copy-start | bytes 393220
  71.4 21.1 %copy-start.1 = (bf16[8,32,2048]{2,1,0:T(8,128)(2,1)S(1)}, bf16[8,32,2048]{2,1,0:T(8,128)(2,1)}, u32[]{:S(2)}) copy-start(bf16[8,32,2048]{2,1,0:T(8,128)(2,1)} %get-tuple-element.8) | copy-start | bytes 3145732
  90.3 2.2 %copy-start.3 = (bf16[2,2048,256]{2,1,0:T(8,128)(2,1)S(1)}, bf16[2,2048,256]{2,1,0:T(8,128)(2,1)}, u32[]{:S(2)}) copy-start(bf16[2,2048,256]{2,1,0:T(8,128)(2,1)} %param.21) | copy-start | bytes 6291460
  100.9 2.2 %copy-start.4 = (bf16[2,2048,256]{2,1,0:T(8,128)(2,1)S(1)}, bf16[2,2048,256]{2,1,0:T(8,128)(2,1)}, u32[]{:S(2)}) copy-start(bf16[2,2048,256]{2,1,0:T(8,128)(2,1)} %param.21) | copy-start | bytes 6291460
  112.1 23.3 %copy-start.2 = (bf16[8,32,2048]{2,1,0:T(8,128)(2,1)S(1)}, bf16[8,32,2048]{2,1,0:T(8,128)(2,1)}, u32[]{:S(2)}) copy-start(bf16[8,32,2048]{2,1,0:T(8,128)(2,1)} %get-tuple-element.6) | copy-start | bytes 3145732
  135.5 2.4 %copy-start.6 = (f32[32,512]{1,0:T(8,128)S(1)}, f32[32,512]{1,0:T(8,128)}, u32[]{:S(2)}) copy-start(f32[32,512]{1,0:T(8,128)} %shard_map.143) | copy-start | bytes 196612
where the time goes:
time: 139 us
  Pallas kernels  95.1 us (68%)
  matrix products  28 us (20%)
  other arithmetic  10.4 us (7%)
  local copies, waits for them, and re-layouts  4.26 us (3%)
    pallas_call x2, Pallas kernels, scatter_sum(): pl.pallas_call(scatter_kernel, out_shape=jax.ShapeDtypeStruct((rows, shar...  45.7 us
    pallas_call x2, Pallas kernels, gather_all(): pl.pallas_call(functools.partial(gather_kernel, n_data, n_meta), out_shap...  44.3 us
    dot_general x4, matrix products, on_device(): lax.dot_general(grad, weight, (((1,), (1,)), ((), ())), preferred_element...  16.4 us
    pallas_call x1, Pallas kernels, swap(): pl.pallas_call(functools.partial(swap_kernel, kind, n), out_shape=jax.Sha...  5.12 us
    dot_general x2, matrix products, on_device(): lax.dot_general(residual_all, w_down[i], (((1,), (1,)), ((), ())), prefer...  4.34 us

commit v1 on v0

v1 whole, which is shorter than its diff:
```python
import functools
import math

import jax
import jax.numpy as jnp
from jax import lax
from jax.experimental import pallas as pl
from jax.experimental.pallas import tpu as pltpu
from jax.sharding import PartitionSpec as P

epsilon = 1e-05
CORES = 2
PAIR = 2
WIDE = 512
MESH = pl.DeviceIdType.MESH
VMEM = pl.BlockSpec(memory_space=pltpu.VMEM)
SMEM = pl.BlockSpec(memory_space=pltpu.SMEM)
ANY = pl.BlockSpec(memory_space=pl.ANY)
f32, bf16 = jnp.float32, jnp.bfloat16
TRANSPOSED = (((1,), (1,)), ((), ()))


def flip(x, mask):
    bit = 1
    while bit <= mask:
        if mask & bit:
            x = x + bit - 2 * bit * ((x // bit) % 2)
        bit *= 2
    return x


def remote(src, dst, send, recv, target):
    return pltpu.make_async_remote_copy(
        src_ref=src, dst_ref=dst, send_sem=send, recv_sem=recv, device_id=target,
        device_id_type=MESH,
    )


def step_kernel(
    layer_ref, moe_ref, gain_ref, head_ref, clean_ref, level_ref, table_ref, gates_ref, ids_ref,
    gate_hbm, up_hbm, down_hbm,
    normed_out, sg_out, residual_out, input_out,
    normed_all, moe_all, res_all, meta_all, meta_t, head, w_gate, w_up, w_down, sg, part, part_0,
    fac_gate, fac_up, y_send, y_recv, z_send, z_recv, own, x_send_1, x_recv_1, x_send_2, x_recv_2,
    res_wide, in_wide, unit, scale,
    ag_send, ag_recv, sib_send, sib_recv, grp_send, grp_recv, p0_send, p0_recv, one_send, one_recv,
    rs_send, rs_recv, x_send_sem, x_recv_sem, local_sem,
):
    e, v = lax.axis_index("expert"), lax.axis_index("vocab")
    n_e, n_v = lax.axis_size("expert"), lax.axis_size("vocab")
    a, c, n_a = v // CORES, v % CORES, n_v // CORES
    o, i, n_o = e // PAIR, e % PAIR, n_e // PAIR
    rows, width = layer_ref.shape
    total_rows = rows * n_e
    vocab_local = head_ref.shape[1]
    local_experts, _, hidden = gate_hbm.shape
    experts_all = local_experts * n_e
    share = width // n_v
    n_g = n_o // 2
    group = 4 * rows
    n_cc = width // WIDE

    def device(o_at, i_at, a_at):
        return (o_at * PAIR + i_at, a_at * CORES + c)

    sibling = (e, a * CORES + 1 - c)
    outer_peer = [device(flip(o, m), i, a) for m in range(n_o)]
    inner_peer = device(o, 1 - i, a)
    chip_peer = [device(o, i, lax.rem(a + d, n_a)) for d in range(n_a)]

    barrier = pltpu.get_barrier_semaphore()
    others = outer_peer[1:] + [inner_peer] + chip_peer[1:] + [sibling]
    for other in others:
        pl.semaphore_signal(barrier, inc=1, device_id=other, device_id_type=MESH)

    def block(m, across):
        at = flip(o, m) * PAIR + (1 - i if across else i)
        return pl.ds(pl.multiple_of(at * rows, rows), rows)

    def group_rows(g):
        return pl.ds(pl.multiple_of(flip(o // 2, g) * group, group), group)

    sends = []

    def start(copy):
        copy.start()
        sends.append(copy)

    def landed(ref, recv):
        remote(ref, ref, recv, recv, sibling).wait_recv()

    def spread(kind, buf, across, m):
        ref = buf.at[block(m, False)]
        if across:
            start(remote(ref, ref, ag_send.at[kind, 1, m], ag_recv.at[kind, 1, m], inner_peer))
        else:
            start(remote(buf.at[block(0, False)], buf.at[block(0, False)], ag_send.at[kind, 0, m],
                         ag_recv.at[kind, 0, m], outer_peer[m]))

    def spread_own(kind, buf):
        for m in range(1, n_o):
            spread(kind, buf, False, m)
            if m == 1:
                spread(kind, buf, True, 0)

    def forward(kind, buf, m):
        landed(buf.at[block(m, False)], ag_recv.at[kind, 0, m])
        spread(kind, buf, True, m)

    def crossed(kind, buf, m):
        landed(buf.at[block(m, True)], ag_recv.at[kind, 1, m])

    def to_sibling(kind, buf, m, across):
        ref, at = buf.at[block(m, across)], 2 * m + across
        start(remote(ref, ref, sib_send.at[kind, at], sib_recv.at[kind, at], sibling))

    def from_sibling(kind, buf, m, across):
        at = 2 * m + across
        landed(buf.at[block(m, across)], sib_recv.at[kind, at])

    loads = [
        pltpu.make_async_copy(gate_hbm, w_gate, local_sem.at[0]),
        pltpu.make_async_copy(up_hbm, w_up, local_sem.at[1]),
        pltpu.make_async_copy(down_hbm, w_down, local_sem.at[2]),
    ]

    def factors(k):
        lane = lax.broadcasted_iota(jnp.int32, (1, meta_all.shape[1]), 1)
        step = math.gcd(total_rows, 256)
        for r in range(0, total_rows, step):
            at = pl.ds(r, step)
            x = moe_all[at, :]
            gate_pre = jnp.dot(x, w_gate[k], preferred_element_type=f32)
            up_pre = jnp.dot(x, w_up[k], preferred_element_type=f32)
            weight = jnp.sum(jnp.where(lane == e * local_experts + k, meta_all[at, :], 0.0),
                             axis=1, keepdims=True)
            s = jax.nn.sigmoid(gate_pre)
            fac_gate[k, at, :] = weight * (up_pre * s * (1.0 + gate_pre * (1.0 - s)))
            fac_up[k, at, :] = weight * (gate_pre * s)

    def hidden_grads(g):
        at = group_rows(g)
        x = res_all[at, :]
        grads = []
        for k in range(local_experts):
            act = lax.dot_general(x, w_down[k], TRANSPOSED, preferred_element_type=f32)
            grads.append((act * fac_gate[k, at, :]).astype(bf16))
            grads.append((act * fac_up[k, at, :]).astype(bf16))
        return grads

    def input_terms(g, grads, j):
        columns = pl.ds(j * WIDE, WIDE)
        term = None
        for k in range(local_experts):
            for grad, weight in ((grads[2 * k], w_gate), (grads[2 * k + 1], w_up)):
                more = lax.dot_general(grad, weight[k, columns, :], TRANSPOSED,
                                       preferred_element_type=f32)
                term = more if term is None else term + more
        part[group_rows(g), columns] = term

    def p0_copy(g, j):
        at, columns = group_rows(g), pl.ds(j * WIDE, WIDE)
        return remote(part.at[at, columns], part_0.at[at, columns], p0_send.at[g, j],
                      p0_recv.at[g, j], sibling)

    def normed_copy(g):
        at = group_rows(g)
        return remote(normed_all.at[at], normed_out.at[at], grp_send.at[0, g], grp_recv.at[0, g],
                      sibling)

    def sg_copy(g):
        at = group_rows(g)
        return remote(sg.at[at, pl.ds(0, vocab_local)], sg_out.at[at], grp_send.at[1, g],
                      grp_recv.at[1, g], sibling)

    head_copy = remote(head_ref, head.at[:, pl.ds(0, vocab_local)], one_send.at[0],
                       one_recv.at[0], sibling)
    meta_copy = remote(meta_all, meta_all, one_send.at[1], one_recv.at[1], sibling)

    def column_share(core):
        return pl.ds(pl.multiple_of((a * CORES + core) * share, share), share)

    residual_copy = remote(res_wide.at[:, column_share(0)], residual_out, one_send.at[2],
                           one_recv.at[2], sibling)
    input_copy = remote(in_wide.at[:, pl.ds(0, share)], input_out, one_send.at[3],
                        one_recv.at[3], sibling)

    @pl.when(c == CORES - 1)
    def _():
        own_head = pltpu.make_async_copy(head_ref, head.at[:, pl.ds(vocab_local, vocab_local)],
                                         local_sem.at[3])
        own_head.start()
        values = layer_ref[...].astype(f32)
        row_scale = jnp.sqrt(jnp.sum(values * values, axis=1, keepdims=True) / width + epsilon)
        unit_rows = values / row_scale
        normed_all[block(0, False), :] = (unit_rows * gain_ref[...]).astype(bf16)
        unit[...] = unit_rows
        scale[...] = jnp.broadcast_to(row_scale, scale.shape)
        meta_t[...] = jnp.zeros_like(meta_t)
        label = lax.broadcasted_iota(jnp.int32, (experts_all, rows), 0)
        gates = jnp.zeros((experts_all, rows), f32)
        for k in range(ids_ref.shape[0]):
            gates = gates + jnp.where(ids_ref[k:k + 1, :] == label, gates_ref[k:k + 1, :], 0.0)
        ratio = jnp.zeros((1, rows), f32)
        for k in range(table_ref.shape[0]):
            ratio = ratio + jnp.where(level_ref[...] == k, table_ref[k], 0.0)
        meta_t[0:experts_all, 0:rows] = gates
        meta_t[experts_all:experts_all + 1, 0:rows] = ratio
        meta_t[experts_all + 1:experts_all + 2, 0:rows] = clean_ref[...].astype(f32)
        meta_all[block(0, False), :] = jnp.transpose(meta_t[...])[0:rows, :]
        pl.semaphore_wait(barrier, len(others))

        spread_own(1, meta_all)
        spread_own(0, normed_all)
        for load in loads:
            load.start()

        def scores(g):
            at = group_rows(g)
            x = normed_all[at, :]
            meta = meta_all[at, :]
            ratio = meta[:, experts_all:experts_all + 1]
            clean = meta[:, experts_all + 1:experts_all + 2]
            wide = math.gcd(2 * vocab_local, 256)
            first = (e * n_v + a * CORES) * vocab_local
            for n in range(0, 2 * vocab_local, wide):
                columns = pl.ds(n, wide)
                score = jnp.dot(x, head[:, columns], preferred_element_type=f32)
                label = first + n + lax.broadcasted_iota(jnp.int32, (1, wide), 1)
                hit = jnp.where(clean == label.astype(f32), ratio, 0.0)
                sg[at, columns] = ((jnp.exp(score) - hit) * (1.0 / math.sqrt(total_rows))).astype(bf16)

        def head_terms(g):
            at = group_rows(g)
            x = sg[at, :]
            for j in range(n_cc):
                columns = pl.ds(j * WIDE, WIDE)
                part[at, columns] = lax.dot_general(x, head[columns, :], TRANSPOSED,
                                                    preferred_element_type=f32)

        def y_copy(q, m):
            return remote(y_send.at[q, m], y_recv.at[q, m], rs_send.at[q, 0, m],
                          rs_recv.at[q, 0, m], inner_peer)

        def z_copy(q, m):
            return remote(z_send.at[q, m], z_recv.at[q, m], rs_send.at[q, 1, m],
                          rs_recv.at[q, 1, m], outer_peer[m])

        def chip_term(q, m, across):
            at = block(m, across)
            return part[at, :] + part_0[at, :] if q else part[at, :]

        def y_step(q, m):
            y_send[q, m] = chip_term(q, m, True).astype(bf16)
            start(y_copy(q, m))

        def z_step(q, m):
            y_copy(q, m).wait_recv()
            term = chip_term(q, m, False) + y_recv[q, m].astype(f32)
            if m:
                z_send[q, m] = term.astype(bf16)
                start(z_copy(q, m))
            else:
                own[...] = term

        def z_sum(q):
            term = own[...]
            for m in range(1, n_o):
                z_copy(q, m).wait_recv()
                term = term + z_recv[q, m].astype(f32)
            return term

        forward(1, meta_all, 1)
        forward(0, normed_all, 1)
        for m in range(2, n_o):
            forward(1, meta_all, m)
        for m in range(n_o):
            crossed(1, meta_all, m)
        start(meta_copy)
        own_head.wait()
        landed(head.at[:, pl.ds(0, vocab_local)], one_recv.at[0])
        ahead = 2
        if ahead < n_o:
            forward(0, normed_all, ahead)
            ahead += 1
        for g in range(n_g):
            for m in (2 * g, 2 * g + 1):
                crossed(0, normed_all, m)
            start(normed_copy(g))
            scores(g)
            start(sg_copy(g))
            for _ in range(2):
                if ahead < n_o:
                    forward(0, normed_all, ahead)
                    ahead += 1
            head_terms(g)
            for m in (2 * g, 2 * g + 1):
                y_step(0, m)
        for m in list(range(1, n_o)) + [0]:
            z_step(0, m)
        keep = [
            pltpu.make_async_copy(normed_all, normed_out, local_sem.at[4]),
            pltpu.make_async_copy(sg.at[:, pl.ds(vocab_local, vocab_local)], sg_out,
                                  local_sem.at[5]),
        ]
        for copy in keep:
            copy.start()
        x_send_1[...] = z_sum(0)
        chips = []
        for d in range(1, n_a):
            copy = remote(x_send_1, x_recv_1.at[d], x_send_sem.at[0, d], x_recv_sem.at[0, d],
                          chip_peer[d])
            start(copy)
            chips.append(copy)
        for load in loads:
            load.wait()
        normed_grad = x_send_1[...]
        for d, copy in enumerate(chips):
            copy.wait_recv()
            normed_grad = normed_grad + x_recv_1[d + 1]
        gained = gain_ref[...] * normed_grad
        mean = jnp.sum(unit[...] * gained, axis=1, keepdims=True) / width
        residual = (gained - unit[...] * mean) / scale[:, 0:1]
        res_all[block(0, False), :] = residual.astype(bf16)
        res_wide[...] = residual
        spread_own(3, res_all)
        to_sibling(1, res_all, 0, False)
        start(residual_copy)
        residual_out[...] = res_wide[:, column_share(1)]
        for m in range(n_o):
            for across in (False, True):
                from_sibling(0, moe_all, m, across)
        half = max(local_experts // 2, 1)
        for k in range(half):
            factors(k)

        def arrive(m):
            forward(3, res_all, m)
            to_sibling(1, res_all, m, False)

        def arrive_across(m):
            crossed(3, res_all, m)
            to_sibling(1, res_all, m, True)

        arrive(1)
        for k in range(half, local_experts):
            factors(k)
        ahead = 2
        if ahead < n_o:
            arrive(ahead)
            ahead += 1
        for g in range(n_g):
            for m in (2 * g, 2 * g + 1):
                arrive_across(m)
            grads = hidden_grads(g)
            for _ in range(2):
                if ahead < n_o:
                    arrive(ahead)
                    ahead += 1
            for j in range(n_cc):
                input_terms(g, grads, j)
            for j in range(n_cc):
                p0_copy(g, j).wait_recv()
            for m in (2 * g, 2 * g + 1):
                y_step(1, m)
        for m in list(range(1, n_o)) + [0]:
            z_step(1, m)
        x_send_2[...] = z_sum(1)
        chips = []
        for d in range(1, n_a):
            at = lax.rem(a + d, n_a)
            columns = pl.ds(pl.multiple_of(at * CORES * share, share), CORES * share)
            copy = remote(x_send_2.at[:, columns], x_recv_2.at[d], x_send_sem.at[1, d],
                          x_recv_sem.at[1, d], chip_peer[d])
            start(copy)
            chips.append(copy)
        total = x_send_2[:, pl.ds(pl.multiple_of(a * CORES * share, share), CORES * share)]
        for d, copy in enumerate(chips):
            copy.wait_recv()
            total = total + x_recv_2[d + 1]
        in_wide[...] = total
        start(input_copy)
        input_out[...] = in_wide[:, pl.ds(share, share)]
        for copy in keep:
            copy.wait()
        for copy in sends:
            copy.wait_send()

    @pl.when(c == 0)
    def _():
        sends.clear()
        own_moe = pltpu.make_async_copy(moe_ref, moe_all.at[block(0, False)], local_sem.at[3])
        own_moe.start()
        for load in loads:
            load.start()
        pl.semaphore_wait(barrier, len(others))
        start(head_copy)
        for g in range(n_g):
            landed(normed_out.at[group_rows(g)], grp_recv.at[0, g])
        own_moe.wait()
        spread_own(2, moe_all)
        to_sibling(0, moe_all, 0, False)
        for m in range(1, n_o):
            forward(2, moe_all, m)
            to_sibling(0, moe_all, m, False)
        for m in range(n_o):
            crossed(2, moe_all, m)
            to_sibling(0, moe_all, m, True)
        for load in loads:
            load.wait()
        landed(meta_all, one_recv.at[1])
        for k in range(local_experts):
            factors(k)
        for g in range(n_g):
            landed(sg_out.at[group_rows(g)], grp_recv.at[1, g])
        for g in range(n_g):
            for m in (2 * g, 2 * g + 1):
                for across in (False, True):
                    from_sibling(1, res_all, m, across)
            grads = hidden_grads(g)
            for j in range(n_cc):
                input_terms(g, grads, j)
                start(p0_copy(g, j))
        landed(residual_out, one_recv.at[2])
        landed(input_out, one_recv.at[3])
        for copy in sends:
            copy.wait_send()


def step(layer_out, moe_input, gain, head_weight, clean, levels, table, gates, ids, w_gate, w_up,
         w_down):
    n_e, n_v = lax.axis_size("expert"), lax.axis_size("vocab")
    n_o, n_a = n_e // PAIR, n_v // CORES
    rows, width = layer_out.shape
    total_rows, share = rows * n_e, width // n_v
    vocab_local = head_weight.shape[1]
    local_experts, _, hidden = w_gate.shape
    lanes = -(-(local_experts * n_e + 2) // 128) * 128
    n_g, n_cc = n_o // 2, width // WIDE
    dma = pltpu.SemaphoreType.DMA
    scratch = [
        pltpu.VMEM((total_rows, width), bf16),
        pltpu.VMEM((total_rows, width), bf16),
        pltpu.VMEM((total_rows, width), bf16),
        pltpu.VMEM((total_rows, lanes), f32),
        pltpu.VMEM((lanes, 128), f32),
        pltpu.VMEM((width, 2 * vocab_local), bf16),
        pltpu.VMEM(w_gate.shape, bf16),
        pltpu.VMEM(w_up.shape, bf16),
        pltpu.VMEM(w_down.shape, bf16),
        pltpu.VMEM((total_rows, 2 * vocab_local), bf16),
        pltpu.VMEM((total_rows, width), f32),
        pltpu.VMEM((total_rows, width), f32),
        pltpu.VMEM((local_experts, total_rows, hidden), f32),
        pltpu.VMEM((local_experts, total_rows, hidden), f32),
        pltpu.VMEM((2, n_o, rows, width), bf16),
        pltpu.VMEM((2, n_o, rows, width), bf16),
        pltpu.VMEM((2, n_o, rows, width), bf16),
        pltpu.VMEM((2, n_o, rows, width), bf16),
        pltpu.VMEM((rows, width), f32),
        pltpu.VMEM((rows, width), f32),
        pltpu.VMEM((n_a, rows, width), f32),
        pltpu.VMEM((rows, width), f32),
        pltpu.VMEM((n_a, rows, CORES * share), f32),
        pltpu.VMEM((rows, width), f32),
        pltpu.VMEM((rows, CORES * share), f32),
        pltpu.VMEM((rows, width), f32),
        pltpu.VMEM((rows, 128), f32),
        dma((4, 2, n_o)), dma((4, 2, n_o)),
        dma((2, 2 * n_o)), dma((2, 2 * n_o)),
        dma((2, n_g)), dma((2, n_g)),
        dma((n_g, n_cc)), dma((n_g, n_cc)),
        dma((4,)), dma((4,)),
        dma((2, 2, n_o)), dma((2, 2, n_o)),
        dma((2, n_a)), dma((2, n_a)),
        dma((6,)),
    ]
    return pl.pallas_call(
        step_kernel,
        out_shape=[
            jax.ShapeDtypeStruct((total_rows, width), bf16),
            jax.ShapeDtypeStruct((total_rows, vocab_local), bf16),
            jax.ShapeDtypeStruct((rows, share), f32),
            jax.ShapeDtypeStruct((rows, share), f32),
        ],
        in_specs=[VMEM, ANY, VMEM, ANY, VMEM, VMEM, SMEM, VMEM, VMEM, ANY, ANY, ANY],
        out_specs=[ANY, ANY, VMEM, VMEM],
        scratch_shapes=scratch,
        compiler_params=pltpu.CompilerParams(
            collective_id=0, has_side_effects=True, vmem_limit_bytes=67043328,
        ),
    )(layer_out, moe_input, gain, head_weight, clean, levels, table, gates, ids, w_gate, w_up,
      w_down)


def on_device(
    layer_out,
    moe_input,
    final_gain,
    head_weight,
    clean_ids,
    levels,
    ratio_table,
    gate_weights,
    expert_ids,
    w_gate,
    w_up,
    w_down,
):
    normed_all, score_grad, residual_grad, input_grad = step(
        layer_out, moe_input, final_gain[None, :], head_weight, clean_ids[None, :],
        levels[None, :], ratio_table, gate_weights.T, expert_ids.T, w_gate, w_up, w_down,
    )
    head_grad = lax.dot_general(
        normed_all, score_grad, (((0,), (0,)), ((), ())), preferred_element_type=jnp.float32
    )
    return (head_grad, residual_grad, input_grad)


def solution(mesh):
    in_specs = (
        P("expert", None),
        P("expert", None),
        P(),
        P(None, ("expert", "vocab")),
        P("expert"),
        P("expert"),
        P(),
        P("expert", None),
        P("expert", None),
        P("expert", None, "vocab"),
        P("expert", None, "vocab"),
        P("expert", "vocab", None),
    )
    out_specs = (P(None, ("expert", "vocab")), P("expert", "vocab"), P("expert", "vocab"))
    return jax.shard_map(
        on_device, mesh=mesh, in_specs=in_specs, out_specs=out_specs, check_vma=False
    )
```

time: 139 us -> 76.3 us (0.55)
  Pallas kernels: 95.1 us -> 70.5 us
  matrix products: 28 us -> 3.69 us
  other arithmetic: 10.4 us -> 0 us
  local copies, waits for them, and re-layouts: 4.26 us -> 1.27 us
    dot_general x10 -> x0, matrix products: 25.6 us -> none  [the longest x4 16.4 us: on_device(): lax.dot_general(grad, weight, (((1,), (1,)), ((), ())), preferred_element...]
    pallas_call x5 -> x1, Pallas kernels: 95.1 us -> 70.5 us  [step(): pl.pallas_call(step_kernel, out_shape=[jax.ShapeDtypeStruct((total_rows,...]
    reduce_sum x5 -> x0, other arithmetic: 4.35 us -> none  [the longest x1 1.04 us: on_device(): jnp.mean(values * values, axis=1, keepdims=True) + epsilon]
    convert_element_type x3 -> x0, other arithmetic: 3.79 us -> none  [the longest x1 1.66 us: on_device(): residual_all, = gather_all([residual_grad.astype(jnp.bfloat16)], [], 5)]
    dynamic_slice x2 -> x0, local copies, waits for them, and re-layouts: 2.25 us -> none  [own_share(): return lax.dynamic_slice_in_dim(x, vocab_at * share, share, axis)]
    slice x2 -> x0, other arithmetic: 1.51 us -> none  [the longest x1 1.33 us: on_device(): gate_all[:, i:i + 1]]
where the time goes in v1:
time: 76.3 us; the launch traced here: 76.1 us
  Pallas kernels  70.5 us (92%)
  matrix products  3.69 us (5%)
  local copies, waits for them, and re-layouts  1.27 us (2%)
    pallas_call x1, Pallas kernels, step(): pl.pallas_call(step_kernel, out_shape=[jax.ShapeDtypeStruct((total_rows,...  70.5 us
    dot_general x1, matrix products, on_device(): lax.dot_general(normed_all, score_grad, (((0,), (0,)), ((), ())), preferr...  3.69 us

profile of v1, /device:TPU:0, one launch (start us, length us, event | category | flops | bytes accessed | tf_op | source)
XLA Modules:
  0.0 76.1 jit_solution(16521615355675046033)
XLA Ops:
  0.6 70.5 %shard_map.139 = (bf16[256,2048]{1,0:T(8,128)(2,1)}, bf16[256,384]{1,0:T(8,128)(2,1)}, f32[32,512]{1,0:T(8,128)}, f32[32,512]{1,0:T(8,128)}) custom-call(bf16[32,2048]{1,0:T(8,128)(2,1)} %layer_ref.1, bf16[32,2048]{1,0:T(8,128)(2,1)} %moe_ref.1, f32[1,2048]{1,0:T(1,128)} %bitcast.7, bf16[2048,384]{1,0:T(8,128)(2,1)} %head_ref.1, s32[1,32]{1,0:T(1,128)} %bitcast.10, ...), custom_call_target="tpu_custom_call" | custom-call | tf_op jit(solution)/shard_map/pallas_call | solution.py:478
  71.1 0.0 copy-start.1
  71.1 0.0 copy-start
  71.2 3.7 %fusion = f32[2048,384]{1,0:T(8,128)} fusion(bf16[256,2048]{1,0:T(8,128)(2,1)} %get-tuple-element.7, bf16[256,384]{1,0:T(8,128)(2,1)} %get-tuple-element.8), kind=kOutput, calls=%fused_computation | convolution fusion | flops 402653184 | bytes 4390912 | tf_op jit(solution)/shard_map/dot_general | solution.py:514
  74.8 0.0 copy-done.1
  74.8 0.6 copy.17
  75.5 0.0 copy-done
  75.5 0.6 copy.18
Async XLA Ops:
  71.1 3.7 %copy-start.1 = (f32[32,512]{1,0:T(8,128)S(1)}, f32[32,512]{1,0:T(8,128)}, u32[]{:S(2)}) copy-start(f32[32,512]{1,0:T(8,128)} %get-tuple-element.15) | copy-start | bytes 196612
  71.1 4.3 %copy-start = (f32[32,512]{1,0:T(8,128)S(1)}, f32[32,512]{1,0:T(8,128)}, u32[]{:S(2)}) copy-start(f32[32,512]{1,0:T(8,128)} %get-tuple-element.16) | copy-start | bytes 196612

commit v2 on v1

v2 whole, which is shorter than its diff:
```python
import functools
import math

import jax
import jax.numpy as jnp
from jax import lax
from jax.experimental import pallas as pl
from jax.experimental.pallas import tpu as pltpu
from jax.sharding import PartitionSpec as P

epsilon = 1e-05
CORES = 2
PAIR = 2
TILE = 256
SPARE = 6 << 20
VMEM_BYTES = 67043328
MESH = pl.DeviceIdType.MESH
ANY = pl.BlockSpec(memory_space=pl.ANY)
VMEM = pl.BlockSpec(memory_space=pltpu.VMEM)
HBM = pl.BlockSpec(memory_space=pltpu.HBM)
f32, bf16 = jnp.float32, jnp.bfloat16
TRANSPOSED = (((1,), (1,)), ((), ()))
META, NORMED, MOE, RES = range(4)
KINDS = 5


def flip(x, mask):
    bit = 1
    while bit <= mask:
        if mask & bit:
            x = x + bit - 2 * bit * ((x // bit) % 2)
        bit *= 2
    return x


def remote(src, dst, send, recv, target):
    return pltpu.make_async_remote_copy(
        src_ref=src, dst_ref=dst, send_sem=send, recv_sem=recv, device_id=target,
        device_id_type=MESH,
    )


def step_kernel(
    layer_hbm, moe_hbm, gain_hbm, head_hbm, clean_hbm, level_hbm, table_hbm, gates_hbm, ids_hbm,
    gate_hbm, up_hbm, down_hbm,
    normed_out, sg_out, residual_out, input_out,
    layer, gain, clean_ids, levels, table, gates, ids,
    normed_all, moe_all, res_all, meta_all, meta_t, head, head_pair, w_both, w_down, act,
    pair_both, sg, sg_pair, grads, grads_pair, part, fac_gate, fac_up,
    xs0, xr0, ys0, yr0, xs1, xr1, ys1, yr1, z_send, z_recv, own, dot_wide, dot_send, dot_recv, dot_chip, dot_outer, scale, unit,
    z_ss, z_rs, y_ss, y_rs, x_ss, x_rs, sib_ss, sib_rs, one_ss, one_rs, wide_ss, wide_rs, pair_ss, pair_rs,
    xs0_s, xs0_r, ys0_s, ys0_r, xs1_s, xs1_r, ys1_s, ys1_r, rz_s, rz_r, dot_s, dot_r, local_sem,
):
    e, v = lax.axis_index("expert"), lax.axis_index("vocab")
    n_e, n_v = lax.axis_size("expert"), lax.axis_size("vocab")
    a, c, n_a = v // CORES, v % CORES, n_v // CORES
    o, i, n_o = e // PAIR, e % PAIR, n_e // PAIR
    rows, width = layer.shape
    total_rows = rows * n_e
    vocab_local = head_hbm.shape[1]
    local_experts, _, hidden = gate_hbm.shape
    experts_all = local_experts * n_e
    share = width // n_v
    cut = share // 2
    row_step = math.gcd(total_rows, 256)
    row_parts = [pl.ds(r, row_step) for r in range(0, total_rows, row_step)]

    def device(o_at, i_at, a_at):
        return (o_at * PAIR + i_at, a_at * CORES + c)

    sibling = (e, a * CORES + 1 - c)
    outer_peer = [device(flip(o, m), i, a) for m in range(n_o)]
    inner_peer = device(o, 1 - i, a)
    chip_at = [lax.rem(a + d, n_a) for d in range(n_a)]
    chip_from = [lax.rem(a + n_a - d, n_a) for d in range(n_a)]
    chip_peer = [device(o, i, chip_at[d]) for d in range(n_a)]
    diagonal_peer = [device(o, 1 - i, chip_at[d]) for d in range(n_a)]

    barrier = pltpu.get_barrier_semaphore()
    others = outer_peer[1:] + [inner_peer] + chip_peer[1:] + diagonal_peer[1:] + [sibling]
    for other in others:
        pl.semaphore_signal(barrier, inc=1, device_id=other, device_id_type=MESH)

    def block(m, across):
        at = flip(o, m) * PAIR + (1 - i if across else i)
        return pl.ds(pl.multiple_of(at * rows, rows), rows)

    def columns_of(at, core):
        return pl.ds(pl.multiple_of((at * CORES + core) * share, share), share)

    def cut_columns(at, s):
        return pl.ds(pl.multiple_of((at * CORES + c) * share + s * cut, cut), cut)

    sends = []

    def start(copy):
        copy.start()
        sends.append(copy)

    def landed(ref, recv):
        remote(ref, ref, recv, recv, sibling).wait_recv()

    def piece(kind, buf, m, across, at, core):
        if kind >= RES:
            first = (at * CORES + core) * share + (kind - RES) * cut
            return buf.at[block(m, across), pl.ds(pl.multiple_of(first, cut), cut)]
        return buf.at[block(m, across), columns_of(at, core)]

    def plane(kind, buf, m):
        ref = piece(kind, buf, m, False, a, c)
        start(remote(ref, ref, y_ss.at[kind, m], y_rs.at[kind, m], inner_peer))
        for d in range(1, n_a):
            if m or kind >= RES:
                start(remote(ref, ref, x_ss.at[kind, 2 * m, d], x_rs.at[kind, 2 * m, d],
                             chip_peer[d]))
            start(remote(ref, ref, x_ss.at[kind, 2 * m + 1, d], x_rs.at[kind, 2 * m + 1, d],
                         diagonal_peer[d]))

    def to_sibling(kind, buf, m, across, d):
        ref, at = piece(kind, buf, m, across, chip_from[d], c), 2 * m + across
        start(remote(ref, ref, sib_ss.at[kind, at, d], sib_rs.at[kind, at, d], sibling))

    def spread(kind, buf):
        ref = piece(kind, buf, 0, False, a, c)
        for m in range(1, n_o):
            start(remote(ref, ref, z_ss.at[kind, m], z_rs.at[kind, m], outer_peer[m]))
        plane(kind, buf, 0)
        if kind >= RES:
            to_sibling(kind, buf, 0, False, 0)

    def forward(kind, buf, m):
        landed(piece(kind, buf, m, False, a, c), z_rs.at[kind, m])
        plane(kind, buf, m)
        to_sibling(kind, buf, m, False, 0)

    def crossed(kind, buf, m):
        landed(piece(kind, buf, m, True, a, c), y_rs.at[kind, m])
        to_sibling(kind, buf, m, True, 0)
        for across in ((False, True) if m or kind >= RES else (True,)):
            for d in range(1, n_a):
                landed(piece(kind, buf, m, across, chip_from[d], c),
                       x_rs.at[kind, 2 * m + across, d])
                to_sibling(kind, buf, m, across, d)

    def from_sibling(kind, buf):
        for m in range(n_o):
            for across in ((False, True) if m or kind >= RES else (True,)):
                for d in range(n_a):
                    landed(piece(kind, buf, m, across, chip_from[d], 1 - c),
                           sib_rs.at[kind, 2 * m + across, d])

    def lanes_of(k, j, n=1):
        return pl.ds((2 * k + j) * hidden, n * hidden)

    down_loads = [
        (down_hbm.at[k], w_down.at[pl.ds(k * hidden, hidden), :]) for k in range(local_experts)
    ]
    own_weights = [
        (src.at[k], w_both.at[:, lanes_of(k, j)])
        for k in range(local_experts) for j, src in enumerate((gate_hbm, up_hbm))
    ]
    loads = [
        pltpu.make_async_copy(src, dst, local_sem.at[k])
        for k, (src, dst) in enumerate((
            (layer_hbm, layer), (gain_hbm, gain), (clean_hbm, clean_ids), (level_hbm, levels),
            (table_hbm, table), (gates_hbm, gates), (ids_hbm, ids), (head_hbm, head),
            (moe_hbm, moe_all.at[block(0, False)]), *down_loads, *own_weights))
    ]
    for copy in loads:
        copy.start()
    meta_t[...] = jnp.zeros_like(meta_t)
    for copy in loads[:7]:
        copy.wait()
    values = layer[...].astype(f32)
    row_scale = jnp.sqrt(jnp.sum(values * values, axis=1, keepdims=True) / width + epsilon)
    unit_rows = values / row_scale
    normed_all[block(0, False), :] = (unit_rows * gain[...]).astype(bf16)
    unit[...] = unit_rows
    scale[...] = jnp.broadcast_to(row_scale, scale.shape)
    label = lax.broadcasted_iota(jnp.int32, (experts_all, rows), 0)
    expert_gates = jnp.zeros((experts_all, rows), f32)
    for k in range(ids.shape[0]):
        expert_gates = expert_gates + jnp.where(ids[k:k + 1, :] == label, gates[k:k + 1, :], 0.0)
    ratio_row = jnp.zeros((1, rows), f32)
    for k in range(table.shape[1]):
        ratio_row = ratio_row + jnp.where(levels[...] == k, table[:, k:k + 1], 0.0)
    meta_t[0:experts_all, 0:rows] = expert_gates
    meta_t[experts_all:experts_all + 1, 0:rows] = ratio_row
    meta_t[experts_all + 1:experts_all + 2, 0:rows] = clean_ids[...].astype(f32)
    meta_all[block(0, False), :] = jnp.transpose(meta_t[...])[0:rows, :]
    pl.semaphore_wait(barrier, len(others))

    def meta_copy(way, m, across=False):
        ref = meta_all.at[block(0 if way == 0 else m, across)]
        if way == 0:
            return remote(ref, ref, z_ss.at[META, m], z_rs.at[META, m], outer_peer[m])
        if way == 1:
            return remote(ref, ref, y_ss.at[META, m], y_rs.at[META, m], inner_peer)
        at = 2 * m + across
        return remote(ref, ref, sib_ss.at[META, at, 0], sib_rs.at[META, at, 0], sibling)

    @pl.when(c == CORES - 1)
    def _():
        for m in range(1, n_o):
            meta_copy(0, m).start()
        meta_copy(1, 0).start()
    spread(NORMED, normed_all)
    head_copies = []
    pair_copies = []
    for d in range(n_a):
        theirs = columns_of(chip_at[d], 1 - c)
        head_copies.append(remote(head_hbm.at[theirs, :], head_pair.at[d], wide_ss.at[0, d],
                                  wide_rs.at[0, d], sibling))
        for k in range(local_experts):
            for j, src in enumerate((gate_hbm, up_hbm)):
                pair_copies.append(remote(
                    src.at[k, theirs, :], pair_both.at[d, :, lanes_of(k, j)],
                    pair_ss.at[d, 2 * k + j], pair_rs.at[d, 2 * k + j], sibling))
    for copy in head_copies + pair_copies:
        start(copy)

    def factors(k):
        lane = lax.broadcasted_iota(jnp.int32, (1, meta_all.shape[1]), 1)
        for at in row_parts:
            x = moe_all[at, :]
            gate_pre = jnp.dot(x, w_both[:, lanes_of(k, 0)], preferred_element_type=f32)
            up_pre = jnp.dot(x, w_both[:, lanes_of(k, 1)], preferred_element_type=f32)
            weight = jnp.sum(jnp.where(lane == e * local_experts + k, meta_all[at, :], 0.0),
                             axis=1, keepdims=True)
            s = jax.nn.sigmoid(gate_pre)
            fac_gate[k, at, :] = weight * (up_pre * s * (1.0 + gate_pre * (1.0 - s)))
            fac_up[k, at, :] = weight * (gate_pre * s)

    act_seen = []

    def act_terms(s, core):
        for d in range(n_a):
            first = pl.multiple_of((chip_at[d] * CORES + core) * share + s * cut, cut)
            columns = pl.ds(first, cut)
            for at in row_parts:
                term = lax.dot_general(res_all[at, columns], w_down[:, columns], TRANSPOSED,
                                       preferred_element_type=f32)
                if act_seen:
                    act[at, :] += term
                else:
                    act[at, :] = term
            act_seen.append(d)

    def hidden_grads(k):
        for at in row_parts:
            own_act = act[at, pl.ds(k * hidden, hidden)]
            grads[at, lanes_of(k, 0)] = (own_act * fac_gate[k, at, :]).astype(bf16)
            grads[at, lanes_of(k, 1)] = (own_act * fac_up[k, at, :]).astype(bf16)

    def grads_copy(k):
        return remote(grads.at[:, lanes_of(k, 0, 2)], grads_pair.at[:, lanes_of(k, 0, 2)],
                      wide_ss.at[1, k], wide_rs.at[1, k], sibling)

    def own_terms(q, d, s):
        columns = cut_columns(chip_at[d], s)
        left, right = (grads, w_both) if q else (sg, head)
        for at in row_parts:
            part[d, s, at, :] = lax.dot_general(left[at, :], right[columns, :], TRANSPOSED,
                                                preferred_element_type=f32)

    def pair_terms(q, d, s):
        columns = pl.ds(s * cut, cut)
        left, right = (grads_pair, pair_both) if q else (sg_pair, head_pair)
        for at in row_parts:
            part[d, s, at, :] += lax.dot_general(left[at, :], right[d, columns, :], TRANSPOSED,
                                                 preferred_element_type=f32)

    def scores():
        for at in row_parts:
            x = normed_all[at, :]
            meta = meta_all[at, :]
            ratio = meta[:, experts_all:experts_all + 1]
            clean = meta[:, experts_all + 1:experts_all + 2]
            score = jnp.dot(x, head[...], preferred_element_type=f32)
            label = (e * n_v + v) * vocab_local + lax.broadcasted_iota(
                jnp.int32, (1, vocab_local), 1)
            hit = jnp.where(clean == label.astype(f32), ratio, 0.0)
            grad = ((jnp.exp(score) - hit) * (1.0 / math.sqrt(total_rows))).astype(bf16)
            sg[at, :] = grad
            dot = jnp.sum(grad.astype(f32) * score, axis=1, keepdims=True)
            dot_wide[at, :] = jnp.broadcast_to(dot, (row_step, 128))
        dot_send[0] = jnp.transpose(dot_wide[...])[0:8, :]

    def x0(q, d):
        return remote(xs0.at[q, d - 1], xr0.at[q, d - 1], xs0_s.at[q, d], xs0_r.at[q, d],
                      chip_peer[d])

    def y0(q):
        return remote(ys0.at[q], yr0.at[q], ys0_s.at[q], ys0_r.at[q], inner_peer)

    def y1(q):
        return remote(ys1.at[q], yr1.at[q], ys1_s.at[q], ys1_r.at[q], inner_peer)

    def x1(q, d):
        return remote(xs1.at[q, d - 1], xr1.at[q, d - 1], xs1_s.at[q, d], xs1_r.at[q, d],
                      chip_peer[d])

    def z(q, s, m):
        return remote(z_send.at[q, s, m], z_recv.at[q, s, m], rz_s.at[q, s, m], rz_r.at[q, s, m],
                      outer_peer[m])

    def terms_and_first(q):
        for d in range(1, n_a):
            pair_terms(q, d, 0)
            xs0[q, d - 1] = part[d, 0].astype(bf16)
            start(x0(q, d))
        for d in range(n_a):
            pair_terms(q, d, 1)
            for m in range(n_o):
                ys1[q, d, m] = part[d, 1, block(m, True), :].astype(bf16)
        start(y1(q))
        pair_terms(q, 0, 0)

    def dot_copies(stage):
        src = dot_send.at[stage]
        if stage == 0:
            return [remote(src, dot_recv.at[0], dot_s.at[0, 0], dot_r.at[0, 0], sibling)]
        if stage == 1:
            return [remote(src, dot_chip.at[d - 1], dot_s.at[1, d], dot_r.at[1, d], chip_peer[d])
                    for d in range(1, n_a)]
        if stage == 2:
            return [remote(src, dot_recv.at[1], dot_s.at[2, 0], dot_r.at[2, 0], inner_peer)]
        return [remote(src, dot_outer.at[m], dot_s.at[3, m], dot_r.at[3, m], outer_peer[m])
                for m in range(1, n_o)]

    def dot_start(stage):
        for copy in dot_copies(stage):
            start(copy)

    def dot_sum(stage):
        for copy in dot_copies(stage):
            copy.wait_recv()
        total = dot_send[stage]
        if stage == 0:
            return total + dot_recv[0]
        if stage == 1:
            for d in range(1, n_a):
                total = total + dot_chip[d - 1]
            return total
        if stage == 2:
            return total + dot_recv[1]
        for m in range(1, n_o):
            total = total + dot_outer[m]
        return total

    def dot_next(stage):
        dot_send[stage + 1] = dot_sum(stage)
        dot_start(stage + 1)

    def second(q):
        for d in range(1, n_a):
            x0(q, d).wait_recv()
        if q == 0:
            dot_next(1)

        def sum_0(m, across):
            at = block(m, across)
            term = part[0, 0, at, :]
            for d in range(1, n_a):
                term = term + xr0[q, d - 1, at, :].astype(f32)
            return term

        for m in range(n_o):
            ys0[q, m] = sum_0(m, True).astype(bf16)
        start(y0(q))
        y1(q).wait_recv()

        def sum_1(d, m):
            return part[d, 1, block(m, False), :] + yr1[q, d, m].astype(f32)

        for d in range(1, n_a):
            for m in range(n_o):
                xs1[q, d - 1, m] = sum_1(d, m).astype(bf16)
            start(x1(q, d))
        return sum_0, sum_1

    def third(q, sum_0, sum_1):
        y0(q).wait_recv()
        if q == 0:
            dot_next(2)
        for m in list(range(1, n_o)) + [0]:
            term = sum_0(m, False) + yr0[q, m].astype(f32)
            if m:
                z_send[q, 0, m] = term
                start(z(q, 0, m))
            else:
                own[0] = term
        for d in range(1, n_a):
            x1(q, d).wait_recv()
        for m in list(range(1, n_o)) + [0]:
            term = sum_1(0, m)
            for d in range(1, n_a):
                term = term + xr1[q, d - 1, m].astype(f32)
            if m:
                z_send[q, 1, m] = term
                start(z(q, 1, m))
            else:
                own[1] = term

    def fourth(q, s):
        term = own[s]
        for m in range(1, n_o):
            z(q, s, m).wait_recv()
            term = term + z_recv[q, s, m]
        return term


    @pl.when(c == CORES - 1)
    def _():
        for m in range(1, n_o):
            landed(meta_all.at[block(m, False)], z_rs.at[META, m])
            meta_copy(1, m).start()
            meta_copy(2, m).start()
    for m in range(1, n_o):
        forward(NORMED, normed_all, m)
    loads[8].wait()
    spread(MOE, moe_all)
    for m in range(n_o):
        crossed(NORMED, normed_all, m)

    @pl.when(c == CORES - 1)
    def _():
        for m in range(n_o):
            landed(meta_all.at[block(m, True)], y_rs.at[META, m])
            meta_copy(2, m, True).start()
        for m in range(n_o):
            if m:
                meta_copy(0, m).wait_send()
                meta_copy(2, m).wait_send()
            meta_copy(1, m).wait_send()
            meta_copy(2, m, True).wait_send()
    for m in range(1, n_o):
        forward(MOE, moe_all, m)

    @pl.when(c == 0)
    def _():
        for m in range(n_o):
            for across in ((False, True) if m else (True,)):
                landed(meta_all.at[block(m, across)], sib_rs.at[META, 2 * m + across, 0])
    loads[7].wait()
    from_sibling(NORMED, normed_all)
    scores()
    sg_copy = remote(sg, sg_pair, one_ss.at[0], one_rs.at[0], sibling)
    start(sg_copy)
    dot_start(0)
    for d in range(n_a):
        for s in range(2):
            own_terms(0, d, s)
    for copy in head_copies:
        copy.wait_recv()
    sg_copy.wait_recv()
    dot_next(0)
    terms_and_first(0)
    for at in row_parts:
        for n in range(0, width, row_step):
            normed_out[pl.ds(n, row_step), at] = jnp.transpose(normed_all[at, pl.ds(n, row_step)])
    sg_out[...] = sg[...]
    sums = second(0)
    for copy in loads[9:]:
        copy.wait()
    third(0, *sums)
    for m in range(n_o):
        crossed(MOE, moe_all, m)
    from_sibling(MOE, moe_all)
    dot_total = dot_sum(3)
    dot_wide[...] = jnp.transpose(jnp.broadcast_to(dot_total[0:1, :], (128, total_rows)))
    mean = dot_wide[block(0, False), 0:1] / width
    own_gain = gain[:, columns_of(a, c)]
    own_unit = unit[:, columns_of(a, c)]
    for s in range(2):
        at = slice(s * cut, (s + 1) * cut)
        residual = (own_gain[:, at] * fourth(0, s) - own_unit[:, at] * mean) / scale[:, 0:1]
        res_all[block(0, False), cut_columns(a, s)] = residual.astype(bf16)
        residual_out[:, at] = residual
        spread(RES + s, res_all)
        for k in range(s, local_experts, 2):
            factors(k)
    for s in range(2):
        for m in range(1, n_o):
            forward(RES + s, res_all, m)
    for s in range(2):
        for m in range(n_o):
            crossed(RES + s, res_all, m)
    from_sibling(RES, res_all)
    act_terms(0, c)
    act_terms(1, c)
    act_terms(0, 1 - c)
    from_sibling(RES + 1, res_all)
    act_terms(1, 1 - c)
    for k in range(local_experts):
        hidden_grads(k)
        start(grads_copy(k))
    for d in range(n_a):
        for s in range(2):
            own_terms(1, d, s)
    for copy in pair_copies:
        copy.wait_recv()
    for k in range(local_experts):
        grads_copy(k).wait_recv()
    terms_and_first(1)
    sums = second(1)
    third(1, *sums)
    for s in range(2):
        input_out[:, s * cut:(s + 1) * cut] = fourth(1, s)
    for copy in sends:
        copy.wait_send()


def step(layer_out, moe_input, gain, head_weight, clean, levels, table, gates, ids, w_gate, w_up,
         w_down):
    n_e, n_v = lax.axis_size("expert"), lax.axis_size("vocab")
    n_o, n_a = n_e // PAIR, n_v // CORES
    rows, width = layer_out.shape
    total_rows, share = rows * n_e, width // n_v
    vocab_local = head_weight.shape[1]
    local_experts, _, hidden = w_gate.shape
    lanes = -(-(local_experts * n_e + 2) // 128) * 128
    cut = share // 2
    more = max(n_a - 1, 1)
    dma = pltpu.SemaphoreType.DMA
    small = (layer_out, gain, clean, levels, table, gates, ids)
    buffers = [pltpu.VMEM(x.shape, x.dtype) for x in small] + [
        pltpu.VMEM((total_rows, width), bf16),
        pltpu.VMEM((total_rows, width), bf16),
        pltpu.VMEM((total_rows, width), bf16),
        pltpu.VMEM((total_rows, lanes), f32),
        pltpu.VMEM((lanes, 128), f32),
        pltpu.VMEM((width, vocab_local), bf16),
        pltpu.VMEM((n_a, share, vocab_local), bf16),
        pltpu.VMEM((width, 2 * local_experts * hidden), bf16),
        pltpu.VMEM((local_experts * hidden, width), bf16),
        pltpu.VMEM((total_rows, local_experts * hidden), f32),
        pltpu.VMEM((n_a, share, 2 * local_experts * hidden), bf16),
        pltpu.VMEM((total_rows, vocab_local), bf16),
        pltpu.VMEM((total_rows, vocab_local), bf16),
        pltpu.VMEM((total_rows, 2 * local_experts * hidden), bf16),
        pltpu.VMEM((total_rows, 2 * local_experts * hidden), bf16),
        pltpu.VMEM((n_a, 2, total_rows, cut), f32),
        pltpu.VMEM((local_experts, total_rows, hidden), f32),
        pltpu.VMEM((local_experts, total_rows, hidden), f32),
        pltpu.VMEM((2, more, total_rows, cut), bf16),
        pltpu.VMEM((2, more, total_rows, cut), bf16),
        pltpu.VMEM((2, n_o, rows, cut), bf16),
        pltpu.VMEM((2, n_o, rows, cut), bf16),
        pltpu.VMEM((2, more, n_o, rows, cut), bf16),
        pltpu.VMEM((2, more, n_o, rows, cut), bf16),
        pltpu.VMEM((2, n_a, n_o, rows, cut), bf16),
        pltpu.VMEM((2, n_a, n_o, rows, cut), bf16),
        pltpu.VMEM((2, 2, n_o, rows, cut), f32),
        pltpu.VMEM((2, 2, n_o, rows, cut), f32),
        pltpu.VMEM((2, rows, cut), f32),
        pltpu.VMEM((total_rows, 128), f32),
        pltpu.VMEM((4, 8, total_rows), f32),
        pltpu.VMEM((2, 8, total_rows), f32),
        pltpu.VMEM((more, 8, total_rows), f32),
        pltpu.VMEM((n_o, 8, total_rows), f32),
        pltpu.VMEM((rows, 128), f32),
        pltpu.VMEM((rows, width), f32),
    ]
    outs = [
        pltpu.VMEM((width, total_rows), bf16),
        pltpu.VMEM((total_rows, vocab_local), bf16),
        pltpu.VMEM((rows, share), f32),
        pltpu.VMEM((rows, share), f32),
    ]
    grant = VMEM_BYTES - sum(math.prod(x.shape) * jnp.dtype(x.dtype).itemsize for x in outs)
    scratch = buffers + [
        dma((KINDS, n_o)), dma((KINDS, n_o)),
        dma((KINDS, n_o)), dma((KINDS, n_o)),
        dma((KINDS, 2 * n_o, n_a)), dma((KINDS, 2 * n_o, n_a)),
        dma((KINDS, 2 * n_o, n_a)), dma((KINDS, 2 * n_o, n_a)),
        dma((1,)), dma((1,)),
        dma((2, max(n_a, local_experts))), dma((2, max(n_a, local_experts))),
        dma((n_a, 2 * local_experts)), dma((n_a, 2 * local_experts)),
        dma((2, n_a)), dma((2, n_a)),
        dma((2,)), dma((2,)),
        dma((2, n_a)), dma((2, n_a)),
        dma((2,)), dma((2,)),
        dma((2, 2, n_o)), dma((2, 2, n_o)),
        dma((4, max(n_a, n_o))), dma((4, max(n_a, n_o))),
        dma((12 + 3 * local_experts,)),
    ]
    return pl.pallas_call(
        step_kernel,
        out_shape=outs,
        in_specs=[HBM] * 12,
        out_specs=[VMEM] * 4,
        scratch_shapes=scratch,
        compiler_params=pltpu.CompilerParams(
            collective_id=0, has_side_effects=True, vmem_limit_bytes=grant,
        ),
    )(layer_out, moe_input, gain, head_weight, clean, levels, table, gates, ids, w_gate, w_up,
      w_down)


def last_kernel(normed_ref, sg_ref, residual_ref, input_ref, head_grad, residual_out, input_out,
                tiles, sems):
    copies = [
        pltpu.make_async_copy(residual_ref, residual_out, sems.at[tiles.shape[0]]),
        pltpu.make_async_copy(input_ref, input_out, sems.at[tiles.shape[0] + 1]),
    ]
    for copy in copies:
        copy.start()
    tile = tiles.shape[1]
    for n in range(tiles.shape[0]):
        at = pl.ds(n * tile, tile)
        tiles[n] = jnp.dot(normed_ref[at, :], sg_ref[...], preferred_element_type=f32)
        copy = pltpu.make_async_copy(tiles.at[n], head_grad.at[at, :], sems.at[n])
        copy.start()
        copies.append(copy)
    for copy in copies:
        copy.wait()


def last(normed, sg, residual, input_grad):
    width = normed.shape[0]
    vocab_local = sg.shape[1]
    tiles = width // TILE
    return pl.pallas_call(
        last_kernel,
        out_shape=[
            jax.ShapeDtypeStruct((width, vocab_local), f32),
            jax.ShapeDtypeStruct(residual.shape, f32),
            jax.ShapeDtypeStruct(input_grad.shape, f32),
        ],
        in_specs=[VMEM] * 4,
        out_specs=[ANY] * 3,
        scratch_shapes=[
            pltpu.VMEM((tiles, TILE, vocab_local), f32),
            pltpu.SemaphoreType.DMA((tiles + 2,)),
        ],
        compiler_params=pltpu.CompilerParams(vmem_limit_bytes=4 * width * vocab_local + SPARE),
    )(*(pltpu.with_memory_space_constraint(x, pltpu.VMEM)
        for x in (normed, sg, residual, input_grad)))


def on_device(
    layer_out,
    moe_input,
    final_gain,
    head_weight,
    clean_ids,
    levels,
    ratio_table,
    gate_weights,
    expert_ids,
    w_gate,
    w_up,
    w_down,
):
    normed_all, score_grad, residual_grad, input_grad = step(
        layer_out, moe_input, final_gain[None, :], head_weight, clean_ids[None, :],
        levels[None, :], ratio_table[None, :], gate_weights.T, expert_ids.T, w_gate, w_up, w_down,
    )
    return tuple(last(normed_all, score_grad, residual_grad, input_grad))


def solution(mesh):
    in_specs = (
        P("expert", None),
        P("expert", None),
        P(),
        P(None, ("expert", "vocab")),
        P("expert"),
        P("expert"),
        P(),
        P("expert", None),
        P("expert", None),
        P("expert", None, "vocab"),
        P("expert", None, "vocab"),
        P("expert", "vocab", None),
    )
    out_specs = (P(None, ("expert", "vocab")), P("expert", "vocab"), P("expert", "vocab"))
    return jax.shard_map(
        on_device, mesh=mesh, in_specs=in_specs, out_specs=out_specs, check_vma=False
    )
```

time: 76.3 us -> 69.8 us (0.915)
  matrix products: 3.69 us -> 0 us
  Pallas kernels: 70.5 us -> 69 us
  local copies, waits for them, and re-layouts: 1.27 us -> 0 us
    dot_general x1 -> x0, matrix products: 3.69 us -> none  [on_device(): lax.dot_general(normed_all, score_grad, (((0,), (0,)), ((), ())), preferr...]
    pallas_call x1 -> x2, Pallas kernels: 70.5 us -> 69 us  [the longest x1 67.1 us: step(): pl.pallas_call(step_kernel, out_shape=outs, in_specs=[HBM] * 12, out_spec...]
    unnamed x6 -> x0, local copies, waits for them, and re-layouts: 1.27 us -> none
where the time goes in v2:
time: 69.8 us; the launch traced here: 69.7 us
  Pallas kernels  69 us (99%)
    pallas_call x1, Pallas kernels, step(): pl.pallas_call(step_kernel, out_shape=outs, in_specs=[HBM] * 12, out_spec...  67.1 us
    pallas_call x1, Pallas kernels, last(): pl.pallas_call(last_kernel, out_shape=[jax.ShapeDtypeStruct((width, vocab...  1.97 us

profile of v2, /device:TPU:0, one launch (start us, length us, event | category | flops | bytes accessed | tf_op | source)
XLA Modules:
  0.0 69.7 jit_solution(9078024253424818630)
XLA Ops:
  0.6 67.1 %shard_map.139 = (bf16[2048,256]{1,0:T(8,128)(2,1)S(1)}, bf16[256,384]{1,0:T(8,128)(2,1)S(1)}, f32[32,512]{1,0:T(8,128)S(1)}, f32[32,512]{1,0:T(8,128)S(1)}) custom-call(bf16[32,2048]{1,0:T(8,128)(2,1)} %layer_hbm.1, bf16[32,2048]{1,0:T(8,128)(2,1)} %moe_hbm.1, f32[1,2048]{1,0:T(1,128)} %bitcast.6, bf16[2048,384]{1,0:T(8,128)(2,1)} %head_hbm.1, ...), custom_call_target="tpu_custom_call" | custom-call | tf_op jit(solution)/shard_map/pallas_call | solution.py:588
  67.7 2.0 %shard_map.140 = (f32[2048,384]{1,0:T(8,128)}, f32[32,512]{1,0:T(8,128)}, f32[32,512]{1,0:T(8,128)}) custom-call(bf16[2048,256]{1,0:T(8,128)(2,1)S(1)} %get-tuple-element.7.normed_ref, bf16[256,384]{1,0:T(8,128)(2,1)S(1)} %get-tuple-element.8.sg_ref, f32[32,512]{1,0:T(8,128)S(1)} %get-tuple-element.9.residual_ref, f32[32,512]{1,0:T(8,128)S(1)} %get-tuple-element.10.input_ref), custom_call_target="tpu_custom_call" | custom-call | tf_op jit(solution)/shard_map/pallas_call | solution.py:624

commit v3 on v2

--- a/solution.py
+++ b/solution.py
@@ -20,8 +20,10 @@
 HBM = pl.BlockSpec(memory_space=pltpu.HBM)
 f32, bf16 = jnp.float32, jnp.bfloat16
 TRANSPOSED = (((1,), (1,)), ((), ()))
-META, NORMED, MOE, RES = range(4)
-KINDS = 5
+NORMED, MOE, RES = range(3)
+KINDS = 4
+X0, Y0, X1, Y1, Z = range(5)
+SG, HEAD, WEIGHTS, GRADS = range(4)
 
 
 def flip(x, mask):
@@ -48,8 +50,8 @@
     normed_all, moe_all, res_all, meta_all, meta_t, head, head_pair, w_both, w_down, act,
     pair_both, sg, sg_pair, grads, grads_pair, part, fac_gate, fac_up,
     xs0, xr0, ys0, yr0, xs1, xr1, ys1, yr1, z_send, z_recv, own, dot_wide, dot_send, dot_recv, dot_chip, dot_outer, scale, unit,
-    z_ss, z_rs, y_ss, y_rs, x_ss, x_rs, sib_ss, sib_rs, one_ss, one_rs, wide_ss, wide_rs, pair_ss, pair_rs,
-    xs0_s, xs0_r, ys0_s, ys0_r, xs1_s, xs1_r, ys1_s, ys1_r, rz_s, rz_r, dot_s, dot_r, local_sem,
+    z_rs, plane_rs, sib_rs, out_ss, meta_z, meta_y, meta_one, one_ss, one_rs, rs_s, rs_r, dot_s,
+    dot_r, local_sem,
 ):
     e, v = lax.axis_index("expert"), lax.axis_index("vocab")
     n_e, n_v = lax.axis_size("expert"), lax.axis_size("vocab")
@@ -91,14 +93,11 @@
     def cut_columns(at, s):
         return pl.ds(pl.multiple_of((at * CORES + c) * share + s * cut, cut), cut)
 
-    sends = []
-
-    def start(copy):
-        copy.start()
-        sends.append(copy)
-
     def landed(ref, recv):
         remote(ref, ref, recv, recv, sibling).wait_recv()
+
+    def left(ref, send):
+        remote(ref, ref, send, send, sibling).wait_send()
 
     def piece(kind, buf, m, across, at, core):
         if kind >= RES:
@@ -106,68 +105,71 @@
             return buf.at[block(m, across), pl.ds(pl.multiple_of(first, cut), cut)]
         return buf.at[block(m, across), columns_of(at, core)]
 
+    def post(kind, ref, recv, target, outer=False):
+        remote(ref, ref, out_ss.at[kind, int(outer and kind >= RES)], recv, target).start()
+
     def plane(kind, buf, m):
         ref = piece(kind, buf, m, False, a, c)
-        start(remote(ref, ref, y_ss.at[kind, m], y_rs.at[kind, m], inner_peer))
         for d in range(1, n_a):
+            post(kind, ref, plane_rs.at[kind, m], diagonal_peer[d])
             if m or kind >= RES:
-                start(remote(ref, ref, x_ss.at[kind, 2 * m, d], x_rs.at[kind, 2 * m, d],
-                             chip_peer[d]))
-            start(remote(ref, ref, x_ss.at[kind, 2 * m + 1, d], x_rs.at[kind, 2 * m + 1, d],
-                         diagonal_peer[d]))
+                post(kind, ref, plane_rs.at[kind, m], chip_peer[d])
+        post(kind, ref, plane_rs.at[kind, m], inner_peer)
 
     def to_sibling(kind, buf, m, across, d):
-        ref, at = piece(kind, buf, m, across, chip_from[d], c), 2 * m + across
-        start(remote(ref, ref, sib_ss.at[kind, at, d], sib_rs.at[kind, at, d], sibling))
+        post(kind, piece(kind, buf, m, across, chip_from[d], c), sib_rs.at[kind], sibling)
 
     def spread(kind, buf):
         ref = piece(kind, buf, 0, False, a, c)
         for m in range(1, n_o):
-            start(remote(ref, ref, z_ss.at[kind, m], z_rs.at[kind, m], outer_peer[m]))
+            post(kind, ref, z_rs.at[kind, m - 1], outer_peer[m], True)
         plane(kind, buf, 0)
         if kind >= RES:
             to_sibling(kind, buf, 0, False, 0)
 
     def forward(kind, buf, m):
-        landed(piece(kind, buf, m, False, a, c), z_rs.at[kind, m])
+        landed(piece(kind, buf, m, False, a, c), z_rs.at[kind, m - 1])
         plane(kind, buf, m)
         to_sibling(kind, buf, m, False, 0)
 
+    def area(kind, buf, height, pieces):
+        return buf.at[pl.ds(0, height * rows), pl.ds(0, pieces * (cut if kind >= RES else share))]
+
     def crossed(kind, buf, m):
-        landed(piece(kind, buf, m, True, a, c), y_rs.at[kind, m])
+        both = m > 0 or kind >= RES
+        landed(area(kind, buf, 1, 2 * n_a - 1 if both else n_a), plane_rs.at[kind, m])
         to_sibling(kind, buf, m, True, 0)
-        for across in ((False, True) if m or kind >= RES else (True,)):
+        for across in ((False, True) if both else (True,)):
             for d in range(1, n_a):
-                landed(piece(kind, buf, m, across, chip_from[d], c),
-                       x_rs.at[kind, 2 * m + across, d])
                 to_sibling(kind, buf, m, across, d)
 
     def from_sibling(kind, buf):
-        for m in range(n_o):
-            for across in ((False, True) if m or kind >= RES else (True,)):
-                for d in range(n_a):
-                    landed(piece(kind, buf, m, across, chip_from[d], 1 - c),
-                           sib_rs.at[kind, 2 * m + across, d])
+        landed(area(kind, buf, 2 * n_o if kind >= RES else 2 * n_o - 1, n_a), sib_rs.at[kind])
+
+    def sent(kind, buf):
+        if kind >= RES:
+            left(area(kind, buf, n_o, 4 * n_a - 1), out_ss.at[kind, 0])
+            left(area(kind, buf, n_o - 1, 1), out_ss.at[kind, 1])
+        else:
+            left(area(kind, buf, 2 * n_o - 1, 2 * n_a), out_ss.at[kind, 0])
 
     def lanes_of(k, j, n=1):
         return pl.ds((2 * k + j) * hidden, n * hidden)
 
-    down_loads = [
-        (down_hbm.at[k], w_down.at[pl.ds(k * hidden, hidden), :]) for k in range(local_experts)
-    ]
-    own_weights = [
-        (src.at[k], w_both.at[:, lanes_of(k, j)])
-        for k in range(local_experts) for j, src in enumerate((gate_hbm, up_hbm))
-    ]
     loads = [
         pltpu.make_async_copy(src, dst, local_sem.at[k])
         for k, (src, dst) in enumerate((
             (layer_hbm, layer), (gain_hbm, gain), (clean_hbm, clean_ids), (level_hbm, levels),
             (table_hbm, table), (gates_hbm, gates), (ids_hbm, ids), (head_hbm, head),
-            (moe_hbm, moe_all.at[block(0, False)]), *down_loads, *own_weights))
+            (moe_hbm, moe_all.at[block(0, False)])))
     ]
     for copy in loads:
         copy.start()
+    for k in range(local_experts):
+        pltpu.make_async_copy(down_hbm.at[k], w_down.at[pl.ds(k * hidden, hidden), :],
+                              local_sem.at[9]).start()
+        for j, src in enumerate((gate_hbm, up_hbm)):
+            pltpu.make_async_copy(src.at[k], w_both.at[:, lanes_of(k, j)], local_sem.at[10]).start()
     meta_t[...] = jnp.zeros_like(meta_t)
     for copy in loads[:7]:
         copy.wait()
@@ -190,34 +192,26 @@
     meta_all[block(0, False), :] = jnp.transpose(meta_t[...])[0:rows, :]
     pl.semaphore_wait(barrier, len(others))
 
-    def meta_copy(way, m, across=False):
-        ref = meta_all.at[block(0 if way == 0 else m, across)]
-        if way == 0:
-            return remote(ref, ref, z_ss.at[META, m], z_rs.at[META, m], outer_peer[m])
-        if way == 1:
-            return remote(ref, ref, y_ss.at[META, m], y_rs.at[META, m], inner_peer)
-        at = 2 * m + across
-        return remote(ref, ref, sib_ss.at[META, at, 0], sib_rs.at[META, at, 0], sibling)
+    def meta_post(m, across, send, recv, target):
+        ref = meta_all.at[block(m, across)]
+        remote(ref, ref, meta_one.at[send], recv, target).start()
 
     @pl.when(c == CORES - 1)
     def _():
         for m in range(1, n_o):
-            meta_copy(0, m).start()
-        meta_copy(1, 0).start()
+            meta_post(0, False, 0, meta_z.at[m - 1], outer_peer[m])
+        meta_post(0, False, 0, meta_y.at[0], inner_peer)
     spread(NORMED, normed_all)
-    head_copies = []
-    pair_copies = []
     for d in range(n_a):
         theirs = columns_of(chip_at[d], 1 - c)
-        head_copies.append(remote(head_hbm.at[theirs, :], head_pair.at[d], wide_ss.at[0, d],
-                                  wide_rs.at[0, d], sibling))
+        remote(head_hbm.at[theirs, :], head_pair.at[d], one_ss.at[HEAD], one_rs.at[HEAD],
+               sibling).start()
+    for d in range(n_a):
+        theirs = columns_of(chip_at[d], 1 - c)
         for k in range(local_experts):
             for j, src in enumerate((gate_hbm, up_hbm)):
-                pair_copies.append(remote(
-                    src.at[k, theirs, :], pair_both.at[d, :, lanes_of(k, j)],
-                    pair_ss.at[d, 2 * k + j], pair_rs.at[d, 2 * k + j], sibling))
-    for copy in head_copies + pair_copies:
-        start(copy)
+                remote(src.at[k, theirs, :], pair_both.at[d, :, lanes_of(k, j)],
+                       one_ss.at[WEIGHTS], one_rs.at[WEIGHTS], sibling).start()
 
     def factors(k):
         lane = lax.broadcasted_iota(jnp.int32, (1, meta_all.shape[1]), 1)
@@ -246,15 +240,12 @@
                     act[at, :] = term
             act_seen.append(d)
 
-    def hidden_grads(k):
-        for at in row_parts:
-            own_act = act[at, pl.ds(k * hidden, hidden)]
-            grads[at, lanes_of(k, 0)] = (own_act * fac_gate[k, at, :]).astype(bf16)
-            grads[at, lanes_of(k, 1)] = (own_act * fac_up[k, at, :]).astype(bf16)
-
-    def grads_copy(k):
-        return remote(grads.at[:, lanes_of(k, 0, 2)], grads_pair.at[:, lanes_of(k, 0, 2)],
-                      wide_ss.at[1, k], wide_rs.at[1, k], sibling)
+    def hidden_grads():
+        for k in range(local_experts):
+            for at in row_parts:
+                own_act = act[at, pl.ds(k * hidden, hidden)]
+                grads[at, lanes_of(k, 0)] = (own_act * fac_gate[k, at, :]).astype(bf16)
+                grads[at, lanes_of(k, 1)] = (own_act * fac_up[k, at, :]).astype(bf16)
 
     def own_terms(q, d, s):
         columns = cut_columns(chip_at[d], s)
@@ -286,55 +277,39 @@
             dot_wide[at, :] = jnp.broadcast_to(dot, (row_step, 128))
         dot_send[0] = jnp.transpose(dot_wide[...])[0:8, :]
 
-    def x0(q, d):
-        return remote(xs0.at[q, d - 1], xr0.at[q, d - 1], xs0_s.at[q, d], xs0_r.at[q, d],
-                      chip_peer[d])
-
-    def y0(q):
-        return remote(ys0.at[q], yr0.at[q], ys0_s.at[q], ys0_r.at[q], inner_peer)
-
-    def y1(q):
-        return remote(ys1.at[q], yr1.at[q], ys1_s.at[q], ys1_r.at[q], inner_peer)
-
-    def x1(q, d):
-        return remote(xs1.at[q, d - 1], xr1.at[q, d - 1], xs1_s.at[q, d], xs1_r.at[q, d],
-                      chip_peer[d])
-
-    def z(q, s, m):
-        return remote(z_send.at[q, s, m], z_recv.at[q, s, m], rz_s.at[q, s, m], rz_r.at[q, s, m],
-                      outer_peer[m])
+    def exchange(q, stage, src, dst, target):
+        remote(src, dst, rs_s.at[q, stage], rs_r.at[q, stage], target).start()
 
     def terms_and_first(q):
         for d in range(1, n_a):
             pair_terms(q, d, 0)
             xs0[q, d - 1] = part[d, 0].astype(bf16)
-            start(x0(q, d))
-        for d in range(n_a):
+            exchange(q, X0, xs0.at[q, d - 1], xr0.at[q, d - 1], chip_peer[d])
+        for d in list(range(1, n_a)) + [0]:
             pair_terms(q, d, 1)
             for m in range(n_o):
                 ys1[q, d, m] = part[d, 1, block(m, True), :].astype(bf16)
-        start(y1(q))
+            exchange(q, Y1, ys1.at[q, d], yr1.at[q, d], inner_peer)
+        own_terms(q, 0, 0)
         pair_terms(q, 0, 0)
 
-    def dot_copies(stage):
+    def dot_start(stage):
         src = dot_send.at[stage]
         if stage == 0:
-            return [remote(src, dot_recv.at[0], dot_s.at[0, 0], dot_r.at[0, 0], sibling)]
-        if stage == 1:
-            return [remote(src, dot_chip.at[d - 1], dot_s.at[1, d], dot_r.at[1, d], chip_peer[d])
-                    for d in range(1, n_a)]
-        if stage == 2:
-            return [remote(src, dot_recv.at[1], dot_s.at[2, 0], dot_r.at[2, 0], inner_peer)]
-        return [remote(src, dot_outer.at[m], dot_s.at[3, m], dot_r.at[3, m], outer_peer[m])
-                for m in range(1, n_o)]
-
-    def dot_start(stage):
-        for copy in dot_copies(stage):
-            start(copy)
+            targets = [(dot_recv.at[0], sibling)]
+        elif stage == 1:
+            targets = [(dot_chip.at[d - 1], chip_peer[d]) for d in range(1, n_a)]
+        elif stage == 2:
+            targets = [(dot_recv.at[1], inner_peer)]
+        else:
+            targets = [(dot_outer.at[m - 1], outer_peer[m]) for m in range(1, n_o)]
+        for dst, target in targets:
+            remote(src, dst, dot_s.at[stage], dot_r.at[stage], target).start()
+
+    dot_whole = [dot_recv.at[0], dot_chip, dot_recv.at[1], dot_outer]
 
     def dot_sum(stage):
-        for copy in dot_copies(stage):
-            copy.wait_recv()
+        landed(dot_whole[stage], dot_r.at[stage])
         total = dot_send[stage]
         if stage == 0:
             return total + dot_recv[0]
@@ -345,7 +320,7 @@
         if stage == 2:
             return total + dot_recv[1]
         for m in range(1, n_o):
-            total = total + dot_outer[m]
+            total = total + dot_outer[m - 1]
         return total
 
     def dot_next(stage):
@@ -353,8 +328,7 @@
         dot_start(stage + 1)
 
     def second(q):
-        for d in range(1, n_a):
-            x0(q, d).wait_recv()
+        landed(xr0.at[q], rs_r.at[q, X0])
         if q == 0:
             dot_next(1)
 
@@ -367,8 +341,8 @@
 
         for m in range(n_o):
             ys0[q, m] = sum_0(m, True).astype(bf16)
-        start(y0(q))
-        y1(q).wait_recv()
+        exchange(q, Y0, ys0.at[q], yr0.at[q], inner_peer)
+        landed(yr1.at[q], rs_r.at[q, Y1])
 
         def sum_1(d, m):
             return part[d, 1, block(m, False), :] + yr1[q, d, m].astype(f32)
@@ -376,84 +350,73 @@
         for d in range(1, n_a):
             for m in range(n_o):
                 xs1[q, d - 1, m] = sum_1(d, m).astype(bf16)
-            start(x1(q, d))
+            exchange(q, X1, xs1.at[q, d - 1], xr1.at[q, d - 1], chip_peer[d])
         return sum_0, sum_1
 
+    def z_post(q, s, m, term):
+        if m:
+            z_send[q, s, m - 1] = term
+            exchange(q, Z + s, z_send.at[q, s, m - 1], z_recv.at[q, s, m - 1], outer_peer[m])
+        else:
+            own[s] = term
+
     def third(q, sum_0, sum_1):
-        y0(q).wait_recv()
+        landed(yr0.at[q], rs_r.at[q, Y0])
         if q == 0:
             dot_next(2)
         for m in list(range(1, n_o)) + [0]:
-            term = sum_0(m, False) + yr0[q, m].astype(f32)
-            if m:
-                z_send[q, 0, m] = term
-                start(z(q, 0, m))
-            else:
-                own[0] = term
-        for d in range(1, n_a):
-            x1(q, d).wait_recv()
+            z_post(q, 0, m, sum_0(m, False) + yr0[q, m].astype(f32))
+        landed(xr1.at[q], rs_r.at[q, X1])
         for m in list(range(1, n_o)) + [0]:
             term = sum_1(0, m)
             for d in range(1, n_a):
                 term = term + xr1[q, d - 1, m].astype(f32)
-            if m:
-                z_send[q, 1, m] = term
-                start(z(q, 1, m))
-            else:
-                own[1] = term
+            z_post(q, 1, m, term)
 
     def fourth(q, s):
+        landed(z_recv.at[q, s], rs_r.at[q, Z + s])
         term = own[s]
         for m in range(1, n_o):
-            z(q, s, m).wait_recv()
-            term = term + z_recv[q, s, m]
+            term = term + z_recv[q, s, m - 1]
         return term
 
-
-    @pl.when(c == CORES - 1)
-    def _():
-        for m in range(1, n_o):
-            landed(meta_all.at[block(m, False)], z_rs.at[META, m])
-            meta_copy(1, m).start()
-            meta_copy(2, m).start()
     for m in range(1, n_o):
+        @pl.when(c == CORES - 1)
+        def _():
+            landed(meta_all.at[block(m, False)], meta_z.at[m - 1])
+            meta_post(m, False, 0, meta_y.at[m], inner_peer)
+            meta_post(m, False, 1, meta_one.at[2], sibling)
         forward(NORMED, normed_all, m)
     loads[8].wait()
     spread(MOE, moe_all)
     for m in range(n_o):
         crossed(NORMED, normed_all, m)
+    meta_area = meta_all.at[pl.ds(0, (2 * n_o - 1) * rows)]
 
     @pl.when(c == CORES - 1)
     def _():
         for m in range(n_o):
-            landed(meta_all.at[block(m, True)], y_rs.at[META, m])
-            meta_copy(2, m, True).start()
-        for m in range(n_o):
-            if m:
-                meta_copy(0, m).wait_send()
-                meta_copy(2, m).wait_send()
-            meta_copy(1, m).wait_send()
-            meta_copy(2, m, True).wait_send()
+            landed(meta_all.at[block(m, True)], meta_y.at[m])
+            meta_post(m, True, 1, meta_one.at[2], sibling)
+        left(meta_area, meta_one.at[0])
+        left(meta_area, meta_one.at[1])
     for m in range(1, n_o):
         forward(MOE, moe_all, m)
 
     @pl.when(c == 0)
     def _():
-        for m in range(n_o):
-            for across in ((False, True) if m else (True,)):
-                landed(meta_all.at[block(m, across)], sib_rs.at[META, 2 * m + across, 0])
+        landed(meta_area, meta_one.at[2])
     loads[7].wait()
     from_sibling(NORMED, normed_all)
     scores()
-    sg_copy = remote(sg, sg_pair, one_ss.at[0], one_rs.at[0], sibling)
-    start(sg_copy)
+    remote(sg, sg_pair, one_ss.at[SG], one_rs.at[SG], sibling).start()
     dot_start(0)
+    for d in range(1, n_a):
+        own_terms(0, d, 0)
     for d in range(n_a):
-        for s in range(2):
-            own_terms(0, d, s)
-    for copy in head_copies:
-        copy.wait_recv()
-    sg_copy.wait_recv()
+        own_terms(0, d, 1)
+    landed(head_pair, one_rs.at[HEAD])
+    landed(sg_pair, one_rs.at[SG])
     dot_next(0)
     terms_and_first(0)
     for at in row_parts:
@@ -461,8 +424,8 @@
             normed_out[pl.ds(n, row_step), at] = jnp.transpose(normed_all[at, pl.ds(n, row_step)])
     sg_out[...] = sg[...]
     sums = second(0)
-    for copy in loads[9:]:
-        copy.wait()
+    pltpu.make_async_copy(w_down, w_down, local_sem.at[9]).wait()
+    pltpu.make_async_copy(w_both, w_both, local_sem.at[10]).wait()
     third(0, *sums)
     for m in range(n_o):
         crossed(MOE, moe_all, m)
@@ -492,23 +455,34 @@
     act_terms(0, 1 - c)
     from_sibling(RES + 1, res_all)
     act_terms(1, 1 - c)
-    for k in range(local_experts):
-        hidden_grads(k)
-        start(grads_copy(k))
+    hidden_grads()
+    remote(grads, grads_pair, one_ss.at[GRADS], one_rs.at[GRADS], sibling).start()
+    for d in range(1, n_a):
+        own_terms(1, d, 0)
     for d in range(n_a):
-        for s in range(2):
-            own_terms(1, d, s)
-    for copy in pair_copies:
-        copy.wait_recv()
-    for k in range(local_experts):
-        grads_copy(k).wait_recv()
+        own_terms(1, d, 1)
+    landed(pair_both, one_rs.at[WEIGHTS])
+    landed(grads_pair, one_rs.at[GRADS])
     terms_and_first(1)
     sums = second(1)
     third(1, *sums)
     for s in range(2):
         input_out[:, s * cut:(s + 1) * cut] = fourth(1, s)
-    for copy in sends:
-        copy.wait_send()
+    sent(NORMED, normed_all)
+    sent(MOE, moe_all)
+    for s in range(2):
+        sent(RES + s, res_all)
+    left(sg, one_ss.at[SG])
+    left(head_pair, one_ss.at[HEAD])
+    left(pair_both, one_ss.at[WEIGHTS])
+    left(grads, one_ss.at[GRADS])
+    for q in range(2):
+        for stage, buf in ((X0, xs0), (Y0, ys0), (X1, xs1), (Y1, ys1)):
+            left(buf.at[q], rs_s.at[q, stage])
+        for s in range(2):
+            left(z_send.at[q, s], rs_s.at[q, Z + s])
+    for stage in range(4):
+        left(dot_whole[stage], dot_s.at[stage])
 
 
 def step(layer_out, moe_input, gain, head_weight, clean, levels, table, gates, ids, w_gate, w_up,
@@ -551,14 +525,14 @@
         pltpu.VMEM((2, more, n_o, rows, cut), bf16),
         pltpu.VMEM((2, n_a, n_o, rows, cut), bf16),
         pltpu.VMEM((2, n_a, n_o, rows, cut), bf16),
-        pltpu.VMEM((2, 2, n_o, rows, cut), f32),
-        pltpu.VMEM((2, 2, n_o, rows, cut), f32),
+        pltpu.VMEM((2, 2, n_o - 1, rows, cut), f32),
+        pltpu.VMEM((2, 2, n_o - 1, rows, cut), f32),
         pltpu.VMEM((2, rows, cut), f32),
         pltpu.VMEM((total_rows, 128), f32),
         pltpu.VMEM((4, 8, total_rows), f32),
         pltpu.VMEM((2, 8, total_rows), f32),
         pltpu.VMEM((more, 8, total_rows), f32),
-        pltpu.VMEM((n_o, 8, total_rows), f32),
+        pltpu.VMEM((n_o - 1, 8, total_rows), f32),
         pltpu.VMEM((rows, 128), f32),
         pltpu.VMEM((rows, width), f32),
     ]
@@ -570,20 +544,12 @@
     ]
     grant = VMEM_BYTES - sum(math.prod(x.shape) * jnp.dtype(x.dtype).itemsize for x in outs)
     scratch = buffers + [
-        dma((KINDS, n_o)), dma((KINDS, n_o)),
-        dma((KINDS, n_o)), dma((KINDS, n_o)),
-        dma((KINDS, 2 * n_o, n_a)), dma((KINDS, 2 * n_o, n_a)),
-        dma((KINDS, 2 * n_o, n_a)), dma((KINDS, 2 * n_o, n_a)),
-        dma((1,)), dma((1,)),
-        dma((2, max(n_a, local_experts))), dma((2, max(n_a, local_experts))),
-        dma((n_a, 2 * local_experts)), dma((n_a, 2 * local_experts)),
-        dma((2, n_a)), dma((2, n_a)),
-        dma((2,)), dma((2,)),
-        dma((2, n_a)), dma((2, n_a)),
-        dma((2,)), dma((2,)),
-        dma((2, 2, n_o)), dma((2, 2, n_o)),
-        dma((4, max(n_a, n_o))), dma((4, max(n_a, n_o))),
-        dma((12 + 3 * local_experts,)),
+        dma((KINDS, n_o - 1)), dma((KINDS, n_o)), dma((KINDS,)), dma((KINDS, 2)),
+        dma((n_o - 1,)), dma((n_o,)), dma((3,)),
+        dma((4,)), dma((4,)),
+        dma((2, 6)), dma((2, 6)),
+        dma((4,)), dma((4,)),
+        dma((11,)),
     ]
     return pl.pallas_call(
         step_kernel,

time: 69.8 us -> 62.7 us (0.90)
  Pallas kernels: 69 us -> 61.9 us
    pallas_call x1, Pallas kernels: 67.1 us -> 60 us  [step(): pl.pallas_call(step_kernel, out_shape=outs, in_specs=[HBM] * 12, out_spec...]
where the time goes in v3:
time: 62.7 us; the launch traced here: 62.6 us
  Pallas kernels  61.9 us (99%)
  between operations  0.64 us (1%)
    pallas_call x1, Pallas kernels, step(): pl.pallas_call(step_kernel, out_shape=outs, in_specs=[HBM] * 12, out_spec...  60 us
    pallas_call x1, Pallas kernels, last(): pl.pallas_call(last_kernel, out_shape=[jax.ShapeDtypeStruct((width, vocab...  1.97 us

profile of v3, /device:TPU:0, one launch (start us, length us, event | category | flops | bytes accessed | tf_op | source)
XLA Modules:
  0.0 62.6 jit_solution(15287685695690523088)
XLA Ops:
  0.6 60.0 %shard_map.139 = (bf16[2048,256]{1,0:T(8,128)(2,1)S(1)}, bf16[256,384]{1,0:T(8,128)(2,1)S(1)}, f32[32,512]{1,0:T(8,128)S(1)}, f32[32,512]{1,0:T(8,128)S(1)}) custom-call(bf16[32,2048]{1,0:T(8,128)(2,1)} %layer_hbm.1, bf16[32,2048]{1,0:T(8,128)(2,1)} %moe_hbm.1, f32[1,2048]{1,0:T(1,128)} %bitcast.6, bf16[2048,384]{1,0:T(8,128)(2,1)} %head_hbm.1, ...), custom_call_target="tpu_custom_call" | custom-call | tf_op jit(solution)/shard_map/pallas_call | solution.py:554
  60.6 2.0 %shard_map.140 = (f32[2048,384]{1,0:T(8,128)}, f32[32,512]{1,0:T(8,128)}, f32[32,512]{1,0:T(8,128)}) custom-call(bf16[2048,256]{1,0:T(8,128)(2,1)S(1)} %get-tuple-element.7.normed_ref, bf16[256,384]{1,0:T(8,128)(2,1)S(1)} %get-tuple-element.8.sg_ref, f32[32,512]{1,0:T(8,128)S(1)} %get-tuple-element.9.residual_ref, f32[32,512]{1,0:T(8,128)S(1)} %get-tuple-element.10.input_ref), custom_call_target="tpu_custom_call" | custom-call | tf_op jit(solution)/shard_map/pallas_call | solution.py:590

commit v4 on v3

--- a/solution.py
+++ b/solution.py
@@ -22,7 +22,6 @@
 TRANSPOSED = (((1,), (1,)), ((), ()))
 NORMED, MOE, RES = range(3)
 KINDS = 4
-X0, Y0, X1, Y1, Z = range(5)
 SG, HEAD, WEIGHTS, GRADS = range(4)
 
 
@@ -49,7 +48,7 @@
     layer, gain, clean_ids, levels, table, gates, ids,
     normed_all, moe_all, res_all, meta_all, meta_t, head, head_pair, w_both, w_down, act,
     pair_both, sg, sg_pair, grads, grads_pair, part, fac_gate, fac_up,
-    xs0, xr0, ys0, yr0, xs1, xr1, ys1, yr1, z_send, z_recv, own, dot_wide, dot_send, dot_recv, dot_chip, dot_outer, scale, unit,
+    p_send, p_recv, z_send_0, z_recv_0, z_send_1, z_recv_1, own, dot_wide, dot_send, dot_recv, dot_chip, dot_outer, scale, unit,
     z_rs, plane_rs, sib_rs, out_ss, meta_z, meta_y, meta_one, one_ss, one_rs, rs_s, rs_r, dot_s,
     dot_r, local_sem,
 ):
@@ -280,104 +279,67 @@
     def exchange(q, stage, src, dst, target):
         remote(src, dst, rs_s.at[q, stage], rs_r.at[q, stage], target).start()
 
+    z_send, z_recv = (z_send_0, z_send_1), (z_recv_0, z_recv_1)
+    corners = [(d, across) for d in range(n_a) for across in (False, True) if d or across]
+    corner_peer = [device(o, 1 - i if across else i, chip_at[d]) for d, across in corners]
+
     def terms_and_first(q):
-        for d in range(1, n_a):
-            pair_terms(q, d, 0)
-            xs0[q, d - 1] = part[d, 0].astype(bf16)
-            exchange(q, X0, xs0.at[q, d - 1], xr0.at[q, d - 1], chip_peer[d])
-        for d in list(range(1, n_a)) + [0]:
-            pair_terms(q, d, 1)
-            for m in range(n_o):
-                ys1[q, d, m] = part[d, 1, block(m, True), :].astype(bf16)
-            exchange(q, Y1, ys1.at[q, d], yr1.at[q, d], inner_peer)
-        own_terms(q, 0, 0)
-        pair_terms(q, 0, 0)
+        for s in range(2):
+            for d in list(range(1, n_a)) + [0]:
+                pair_terms(q, d, s)
+                for j, (to, across) in enumerate(corners):
+                    if to == d:
+                        for m in range(n_o):
+                            p_send[q, s, j, m] = part[d, s, block(m, across), :].astype(bf16)
+                        exchange(q, s, p_send.at[q, s, j], p_recv.at[q, s, j], corner_peer[j])
 
     def dot_start(stage):
         src = dot_send.at[stage]
         if stage == 0:
-            targets = [(dot_recv.at[0], sibling)]
+            targets = [(dot_recv, sibling)]
         elif stage == 1:
-            targets = [(dot_chip.at[d - 1], chip_peer[d]) for d in range(1, n_a)]
-        elif stage == 2:
-            targets = [(dot_recv.at[1], inner_peer)]
+            targets = [(dot_chip.at[j], peer) for j, peer in enumerate(corner_peer)]
         else:
             targets = [(dot_outer.at[m - 1], outer_peer[m]) for m in range(1, n_o)]
         for dst, target in targets:
             remote(src, dst, dot_s.at[stage], dot_r.at[stage], target).start()
 
-    dot_whole = [dot_recv.at[0], dot_chip, dot_recv.at[1], dot_outer]
+    dot_whole = [dot_recv, dot_chip, dot_outer]
 
     def dot_sum(stage):
         landed(dot_whole[stage], dot_r.at[stage])
         total = dot_send[stage]
         if stage == 0:
-            return total + dot_recv[0]
-        if stage == 1:
-            for d in range(1, n_a):
-                total = total + dot_chip[d - 1]
-            return total
-        if stage == 2:
-            return total + dot_recv[1]
-        for m in range(1, n_o):
-            total = total + dot_outer[m - 1]
+            return total + dot_recv[...]
+        for j in range(dot_whole[stage].shape[0]):
+            total = total + dot_whole[stage][j]
         return total
 
     def dot_next(stage):
         dot_send[stage + 1] = dot_sum(stage)
         dot_start(stage + 1)
 
-    def second(q):
-        landed(xr0.at[q], rs_r.at[q, X0])
-        if q == 0:
-            dot_next(1)
-
-        def sum_0(m, across):
-            at = block(m, across)
-            term = part[0, 0, at, :]
-            for d in range(1, n_a):
-                term = term + xr0[q, d - 1, at, :].astype(f32)
-            return term
-
-        for m in range(n_o):
-            ys0[q, m] = sum_0(m, True).astype(bf16)
-        exchange(q, Y0, ys0.at[q], yr0.at[q], inner_peer)
-        landed(yr1.at[q], rs_r.at[q, Y1])
-
-        def sum_1(d, m):
-            return part[d, 1, block(m, False), :] + yr1[q, d, m].astype(f32)
-
-        for d in range(1, n_a):
-            for m in range(n_o):
-                xs1[q, d - 1, m] = sum_1(d, m).astype(bf16)
-            exchange(q, X1, xs1.at[q, d - 1], xr1.at[q, d - 1], chip_peer[d])
-        return sum_0, sum_1
-
-    def z_post(q, s, m, term):
-        if m:
-            z_send[q, s, m - 1] = term
-            exchange(q, Z + s, z_send.at[q, s, m - 1], z_recv.at[q, s, m - 1], outer_peer[m])
-        else:
-            own[s] = term
-
-    def third(q, sum_0, sum_1):
-        landed(yr0.at[q], rs_r.at[q, Y0])
-        if q == 0:
-            dot_next(2)
-        for m in list(range(1, n_o)) + [0]:
-            z_post(q, 0, m, sum_0(m, False) + yr0[q, m].astype(f32))
-        landed(xr1.at[q], rs_r.at[q, X1])
-        for m in list(range(1, n_o)) + [0]:
-            term = sum_1(0, m)
-            for d in range(1, n_a):
-                term = term + xr1[q, d - 1, m].astype(f32)
-            z_post(q, 1, m, term)
+    def third(q):
+        for s in range(2):
+            landed(p_recv.at[q, s], rs_r.at[q, s])
+            if q == 0 and s == 0:
+                dot_next(1)
+            for m in list(range(2, n_o)) + [1, 0]:
+                term = part[0, s, block(m, False), :]
+                for j in range(len(corners)):
+                    term = term + p_recv[q, s, j, m].astype(f32)
+                if m:
+                    z_send[q][s, m - 1] = term.astype(z_send[q].dtype)
+                    exchange(q, 2 + s, z_send[q].at[s, m - 1], z_recv[q].at[s, m - 1],
+                             outer_peer[m])
+                else:
+                    own[s] = term
 
     def fourth(q, s):
-        landed(z_recv.at[q, s], rs_r.at[q, Z + s])
+        landed(z_recv[q].at[s], rs_r.at[q, 2 + s])
         term = own[s]
         for m in range(1, n_o):
-            term = term + z_recv[q, s, m - 1]
+            term = term + z_recv[q][s, m - 1].astype(f32)
         return term
 
     for m in range(1, n_o):
@@ -411,10 +373,9 @@
     scores()
     remote(sg, sg_pair, one_ss.at[SG], one_rs.at[SG], sibling).start()
     dot_start(0)
-    for d in range(1, n_a):
-        own_terms(0, d, 0)
-    for d in range(n_a):
-        own_terms(0, d, 1)
+    for s in range(2):
+        for d in list(range(1, n_a)) + [0]:
+            own_terms(0, d, s)
     landed(head_pair, one_rs.at[HEAD])
     landed(sg_pair, one_rs.at[SG])
     dot_next(0)
@@ -423,14 +384,13 @@
         for n in range(0, width, row_step):
             normed_out[pl.ds(n, row_step), at] = jnp.transpose(normed_all[at, pl.ds(n, row_step)])
     sg_out[...] = sg[...]
-    sums = second(0)
     pltpu.make_async_copy(w_down, w_down, local_sem.at[9]).wait()
     pltpu.make_async_copy(w_both, w_both, local_sem.at[10]).wait()
-    third(0, *sums)
+    third(0)
     for m in range(n_o):
         crossed(MOE, moe_all, m)
     from_sibling(MOE, moe_all)
-    dot_total = dot_sum(3)
+    dot_total = dot_sum(2)
     dot_wide[...] = jnp.transpose(jnp.broadcast_to(dot_total[0:1, :], (128, total_rows)))
     mean = dot_wide[block(0, False), 0:1] / width
     own_gain = gain[:, columns_of(a, c)]
@@ -457,15 +417,13 @@
     act_terms(1, 1 - c)
     hidden_grads()
     remote(grads, grads_pair, one_ss.at[GRADS], one_rs.at[GRADS], sibling).start()
-    for d in range(1, n_a):
-        own_terms(1, d, 0)
-    for d in range(n_a):
-        own_terms(1, d, 1)
+    for s in range(2):
+        for d in list(range(1, n_a)) + [0]:
+            own_terms(1, d, s)
     landed(pair_both, one_rs.at[WEIGHTS])
     landed(grads_pair, one_rs.at[GRADS])
     terms_and_first(1)
-    sums = second(1)
-    third(1, *sums)
+    third(1)
     for s in range(2):
         input_out[:, s * cut:(s + 1) * cut] = fourth(1, s)
     sent(NORMED, normed_all)
@@ -477,11 +435,10 @@
     left(pair_both, one_ss.at[WEIGHTS])
     left(grads, one_ss.at[GRADS])
     for q in range(2):
-        for stage, buf in ((X0, xs0), (Y0, ys0), (X1, xs1), (Y1, ys1)):
-            left(buf.at[q], rs_s.at[q, stage])
         for s in range(2):
-            left(z_send.at[q, s], rs_s.at[q, Z + s])
-    for stage in range(4):
+            left(p_send.at[q, s], rs_s.at[q, s])
+            left(z_send[q].at[s], rs_s.at[q, 2 + s])
+    for stage in range(3):
         left(dot_whole[stage], dot_s.at[stage])
 
 
@@ -495,7 +452,6 @@
     local_experts, _, hidden = w_gate.shape
     lanes = -(-(local_experts * n_e + 2) // 128) * 128
     cut = share // 2
-    more = max(n_a - 1, 1)
     dma = pltpu.SemaphoreType.DMA
     small = (layer_out, gain, clean, levels, table, gates, ids)
     buffers = [pltpu.VMEM(x.shape, x.dtype) for x in small] + [
@@ -517,21 +473,17 @@
         pltpu.VMEM((n_a, 2, total_rows, cut), f32),
         pltpu.VMEM((local_experts, total_rows, hidden), f32),
         pltpu.VMEM((local_experts, total_rows, hidden), f32),
-        pltpu.VMEM((2, more, total_rows, cut), bf16),
-        pltpu.VMEM((2, more, total_rows, cut), bf16),
-        pltpu.VMEM((2, n_o, rows, cut), bf16),
-        pltpu.VMEM((2, n_o, rows, cut), bf16),
-        pltpu.VMEM((2, more, n_o, rows, cut), bf16),
-        pltpu.VMEM((2, more, n_o, rows, cut), bf16),
-        pltpu.VMEM((2, n_a, n_o, rows, cut), bf16),
-        pltpu.VMEM((2, n_a, n_o, rows, cut), bf16),
-        pltpu.VMEM((2, 2, n_o - 1, rows, cut), f32),
-        pltpu.VMEM((2, 2, n_o - 1, rows, cut), f32),
+        pltpu.VMEM((2, 2, 2 * n_a - 1, n_o, rows, cut), bf16),
+        pltpu.VMEM((2, 2, 2 * n_a - 1, n_o, rows, cut), bf16),
+        pltpu.VMEM((2, n_o - 1, rows, cut), bf16),
+        pltpu.VMEM((2, n_o - 1, rows, cut), bf16),
+        pltpu.VMEM((2, n_o - 1, rows, cut), f32),
+        pltpu.VMEM((2, n_o - 1, rows, cut), f32),
         pltpu.VMEM((2, rows, cut), f32),
         pltpu.VMEM((total_rows, 128), f32),
-        pltpu.VMEM((4, 8, total_rows), f32),
-        pltpu.VMEM((2, 8, total_rows), f32),
-        pltpu.VMEM((more, 8, total_rows), f32),
+        pltpu.VMEM((3, 8, total_rows), f32),
+        pltpu.VMEM((8, total_rows), f32),
+        pltpu.VMEM((2 * n_a - 1, 8, total_rows), f32),
         pltpu.VMEM((n_o - 1, 8, total_rows), f32),
         pltpu.VMEM((rows, 128), f32),
         pltpu.VMEM((rows, width), f32),
@@ -547,8 +499,8 @@
         dma((KINDS, n_o - 1)), dma((KINDS, n_o)), dma((KINDS,)), dma((KINDS, 2)),
         dma((n_o - 1,)), dma((n_o,)), dma((3,)),
         dma((4,)), dma((4,)),
-        dma((2, 6)), dma((2, 6)),
-        dma((4,)), dma((4,)),
+        dma((2, 4)), dma((2, 4)),
+        dma((3,)), dma((3,)),
         dma((11,)),
     ]
     return pl.pallas_call(

time: 62.7 us -> 58.2 us (0.928)
  Pallas kernels: 61.9 us -> 57.4 us
    pallas_call x1, Pallas kernels: 60 us -> 55.5 us  [step(): pl.pallas_call(step_kernel, out_shape=outs, in_specs=[HBM] * 12, out_spec...]
where the time goes in v4:
time: 58.2 us; the launch traced here: 58.1 us
  Pallas kernels  57.4 us (99%)
  between operations  0.64 us (1%)
    pallas_call x1, Pallas kernels, step(): pl.pallas_call(step_kernel, out_shape=outs, in_specs=[HBM] * 12, out_spec...  55.5 us
    pallas_call x1, Pallas kernels, last(): pl.pallas_call(last_kernel, out_shape=[jax.ShapeDtypeStruct((width, vocab...  1.97 us

profile of v4, /device:TPU:0, one launch (start us, length us, event | category | flops | bytes accessed | tf_op | source)
XLA Modules:
  0.0 58.1 jit_solution(17256126257202859926)
XLA Ops:
  0.6 55.5 %shard_map.139 = (bf16[2048,256]{1,0:T(8,128)(2,1)S(1)}, bf16[256,384]{1,0:T(8,128)(2,1)S(1)}, f32[32,512]{1,0:T(8,128)S(1)}, f32[32,512]{1,0:T(8,128)S(1)}) custom-call(bf16[32,2048]{1,0:T(8,128)(2,1)} %layer_hbm.1, bf16[32,2048]{1,0:T(8,128)(2,1)} %moe_hbm.1, f32[1,2048]{1,0:T(1,128)} %bitcast.6, bf16[2048,384]{1,0:T(8,128)(2,1)} %head_hbm.1, ...), custom_call_target="tpu_custom_call" | custom-call | tf_op jit(solution)/shard_map/pallas_call | solution.py:506
  56.1 2.0 %shard_map.140 = (f32[2048,384]{1,0:T(8,128)}, f32[32,512]{1,0:T(8,128)}, f32[32,512]{1,0:T(8,128)}) custom-call(bf16[2048,256]{1,0:T(8,128)(2,1)S(1)} %get-tuple-element.7.normed_ref, bf16[256,384]{1,0:T(8,128)(2,1)S(1)} %get-tuple-element.8.sg_ref, f32[32,512]{1,0:T(8,128)S(1)} %get-tuple-element.9.residual_ref, f32[32,512]{1,0:T(8,128)S(1)} %get-tuple-element.10.input_ref), custom_call_target="tpu_custom_call" | custom-call | tf_op jit(solution)/shard_map/pallas_call | solution.py:542

commit v5 on v4

--- a/solution.py
+++ b/solution.py
@@ -110,7 +110,11 @@
     def plane(kind, buf, m):
         ref = piece(kind, buf, m, False, a, c)
         for d in range(1, n_a):
-            post(kind, ref, plane_rs.at[kind, m], diagonal_peer[d])
+            if m or kind >= RES:
+                post(kind, ref, plane_rs.at[kind, m], diagonal_peer[d])
+            else:
+                post(kind, piece(kind, buf, 0, False, chip_at[d], c), plane_rs.at[kind, m],
+                     inner_peer)
             if m or kind >= RES:
                 post(kind, ref, plane_rs.at[kind, m], chip_peer[d])
         post(kind, ref, plane_rs.at[kind, m], inner_peer)
@@ -353,6 +357,8 @@
     spread(MOE, moe_all)
     for m in range(n_o):
         crossed(NORMED, normed_all, m)
+        if m:
+            forward(MOE, moe_all, m)
     meta_area = meta_all.at[pl.ds(0, (2 * n_o - 1) * rows)]
 
     @pl.when(c == CORES - 1)
@@ -362,8 +368,6 @@
             meta_post(m, True, 1, meta_one.at[2], sibling)
         left(meta_area, meta_one.at[0])
         left(meta_area, meta_one.at[1])
-    for m in range(1, n_o):
-        forward(MOE, moe_all, m)
 
     @pl.when(c == 0)
     def _():

time: 58.2 us -> 57.2 us (0.983)
  Pallas kernels: 57.4 us -> 56.4 us
    pallas_call x1, Pallas kernels: 55.5 us -> 54.4 us  [step(): pl.pallas_call(step_kernel, out_shape=outs, in_specs=[HBM] * 12, out_spec...]
where the time goes in v5:
time: 57.2 us; the launch traced here: 57 us
  Pallas kernels  56.4 us (99%)
  between operations  0.64 us (1%)
    pallas_call x1, Pallas kernels, step(): pl.pallas_call(step_kernel, out_shape=outs, in_specs=[HBM] * 12, out_spec...  54.4 us
    pallas_call x1, Pallas kernels, last(): pl.pallas_call(last_kernel, out_shape=[jax.ShapeDtypeStruct((width, vocab...  1.97 us

profile of v5, /device:TPU:0, one launch (start us, length us, event | category | flops | bytes accessed | tf_op | source)
XLA Modules:
  0.0 57.0 jit_solution(4372724639923843105)
XLA Ops:
  0.6 54.4 %shard_map.139 = (bf16[2048,256]{1,0:T(8,128)(2,1)S(1)}, bf16[256,384]{1,0:T(8,128)(2,1)S(1)}, f32[32,512]{1,0:T(8,128)S(1)}, f32[32,512]{1,0:T(8,128)S(1)}) custom-call(bf16[32,2048]{1,0:T(8,128)(2,1)} %layer_hbm.1, bf16[32,2048]{1,0:T(8,128)(2,1)} %moe_hbm.1, f32[1,2048]{1,0:T(1,128)} %bitcast.6, bf16[2048,384]{1,0:T(8,128)(2,1)} %head_hbm.1, ...), custom_call_target="tpu_custom_call" | custom-call | tf_op jit(solution)/shard_map/pallas_call | solution.py:510
  55.1 2.0 %shard_map.140 = (f32[2048,384]{1,0:T(8,128)}, f32[32,512]{1,0:T(8,128)}, f32[32,512]{1,0:T(8,128)}) custom-call(bf16[2048,256]{1,0:T(8,128)(2,1)S(1)} %get-tuple-element.7.normed_ref, bf16[256,384]{1,0:T(8,128)(2,1)S(1)} %get-tuple-element.8.sg_ref, f32[32,512]{1,0:T(8,128)S(1)} %get-tuple-element.9.residual_ref, f32[32,512]{1,0:T(8,128)S(1)} %get-tuple-element.10.input_ref), custom_call_target="tpu_custom_call" | custom-call | tf_op jit(solution)/shard_map/pallas_call | solution.py:546
